TPU v7x, 32 devices: a whole 2x2x4 slice. The times are simulated.
32 devices in a mesh: dp: 8 (over y, x, core), expert: 4 (over z).
Axes of the slice: x: 2, y: 2, z: 4, core: 2. Of those that a mesh axis runs over, the one named last changes fastest.
Arguments:
- tokens: bfloat16 [4096, 1792], P(('dp', 'expert')), may hold values from -6 to 6
- routes: int32 [4096, 2], P(('dp', 'expert')), may hold values from 0 to 3, all different within a row; in each aligned block of 128 rows (0 to 127, 128 to 255, ...) at most 128 rows name the same one
- gates: float32 [4096, 2], P(('dp', 'expert')), may hold values from 0.25 to 1
- grad_hidden: bfloat16 [4096, 2, 512], P(('dp', 'expert')), may hold values from -4 to 4
- w_in: bfloat16 [4, 1792, 512], P('expert', 'dp'), may hold values from -0.25 to 0.25
- error: bfloat16 [8, 4, 1792, 512], P('dp', 'expert'), may hold values from -6 to 6
- q_seed: float32 [4, 512, 32], P('expert'), may hold values from -6 to 6
Outputs:
- grad_tokens: bfloat16 [4096, 1792], P(('dp', 'expert'))
- error_next: bfloat16 [8, 4, 1792, 512], P('dp', 'expert')
- weight_grad: float32 [4, 1792, 512], P('expert', 'dp')
Inputs may be any that keep to these rules, and one draw needn't show every extreme that they name: `routes`: in the rows of one device no expert is named by more than 128 rows, a bound that some block reaches; the two experts of a row differ.
All inputs are finite; a program needn't handle non-finite values.
Results may differ from a plain program's by a relative error of at most 0.014.
Values may be sent and summed in bfloat16 or wider, within the bound.
A program may use at most 64 MiB of HBM per device.

v0:
```python
import functools

import jax
import jax.numpy as jnp
from jax import lax
from jax.experimental import pallas as pl
from jax.experimental.pallas import tpu as pltpu
from jax.sharding import PartitionSpec as P

HI = lax.Precision.HIGHEST
MESH = pl.DeviceIdType.MESH
F32 = jnp.float32
BF16 = jnp.bfloat16


def slopes(pre_act):
    squashed = 1.0 / (1.0 + jnp.exp(-pre_act))
    return squashed * (1.0 + pre_act * (1.0 - squashed))


def inverse_factor(gram):
    rank = gram.shape[0]
    rows = lax.broadcasted_iota(jnp.int32, (rank, rank), 0)
    cols = lax.broadcasted_iota(jnp.int32, (rank, rank), 1)
    left = gram
    right = (rows == cols).astype(F32)
    row_id = lax.broadcasted_iota(jnp.int32, (rank, 1), 0)
    for i in range(rank - 1):
        scale = 1.0 / left[i : i + 1, i : i + 1]
        col = jnp.where(row_id > i, left[:, i : i + 1], 0.0)
        row_l = left[i : i + 1, :] * scale
        row_r = right[i : i + 1, :] * scale
        left = left - col * row_l
        right = right - col * row_r
    pivots = jnp.sum(jnp.where(rows == cols, left, 0.0), axis=1, keepdims=True)
    return right * (1.0 / jnp.sqrt(pivots))


def kernel(dims, tok_ref, gh_ref, gate_ref, w_ref, err_hbm, qt_ref,
           gt_out, err_out, wg_out,
           tok_all, gh_all, gate_all, w_all, x_all, gp_all, err_v, merged, back, ret,
           facc, fbuf, rsbuf, agbuf, tbuf,
           err_sem, tok_s, tok_r, gh_s, gh_r, gate_s, gate_r, w_s, w_r,
           f_s, f_r, a_s, a_r, t_s, t_r, b_s, b_r):
    E, N, rp, chunk, gather_w = dims
    z = lax.axis_index("expert")
    me = lax.axis_index("dp")
    tokens, width = tok_ref.shape
    shard = width // N
    rank = qt_ref.shape[0]
    groups = width // 128

    def other(axis, size, k):
        return lax.rem(lax.axis_index(axis) + k, size)

    def loop(size, fn, start=1):
        def step(k, c):
            fn(k)
            return c
        lax.fori_loop(start, size, step, 0)

    err_copy = pltpu.make_async_copy(err_hbm.at[0, 0], err_v, err_sem)
    err_copy.start()

    barrier = pltpu.get_barrier_semaphore()
    loop(E, lambda k: pl.semaphore_signal(
        barrier, inc=1, device_id={"expert": other("expert", E, k)}, device_id_type=MESH))
    loop(N, lambda k: pl.semaphore_signal(
        barrier, inc=1, device_id={"dp": other("dp", N, k)}, device_id_type=MESH))
    pl.semaphore_wait(barrier, E - 1 + N - 1)

    def rdma(src, dst, s, r, axis, peer):
        return pltpu.make_async_remote_copy(
            src_ref=src, dst_ref=dst, send_sem=s, recv_sem=r,
            device_id={axis: peer}, device_id_type=MESH)

    def gate_copy(p, slot, k):
        return rdma(gate_ref.at[p], gate_all.at[slot], gate_s.at[k], gate_r.at[slot], "expert", p)

    def gh_copy(p, slot, k):
        return rdma(gh_ref.at[p], gh_all.at[slot], gh_s.at[k], gh_r.at[slot], "expert", p)

    def tok_copy(j, nb, slot):
        src = tok_all.at[j]
        return rdma(src, tok_all.at[j], tok_s.at[slot], tok_r.at[j], "expert", nb)

    def w_copy(p, slot, k):
        return rdma(w_ref, w_all.at[pl.ds(pl.multiple_of(slot * shard, 16), shard)],
                    w_s.at[k], w_r.at[slot], "dp", p)

    def each(p_axis, size, copy, act):
        mine = lax.axis_index(p_axis)

        def fn(k):
            p = other(p_axis, size, k)
            if act == "start":
                copy(p, mine, k).start()
            elif act == "recv":
                copy(p, p, k).wait_recv()
            else:
                copy(p, mine, k).wait_send()
        loop(size, fn)

    def forward(s, mode):
        for d, dirn in enumerate((1, -1)):
            j = z - dirn * s
            nb = z + dirn
            inside = (j >= 0) & (j < E)
            linked = inside & (nb >= 0) & (nb < E)
            slot = d * E + s
            if mode == "first":
                @pl.when(linked)
                def _():
                    rdma(tok_ref, tok_all.at[z], tok_s.at[slot], tok_r.at[z], "expert", nb).start()
            elif mode == "relay":
                @pl.when(inside)
                def _():
                    tok_copy(j, nb, slot).wait_recv()

                @pl.when(linked)
                def _():
                    tok_copy(j, nb, slot).start()
            else:
                @pl.when(linked)
                def _():
                    tok_copy(j, nb, slot).wait_send()

    each("expert", E, gate_copy, "start")
    forward(0, "first")
    each("expert", E, gh_copy, "start")
    if gather_w:
        each("dp", N, w_copy, "start")
        w_all[pl.ds(pl.multiple_of(me * shard, 16), shard), :] = w_ref[...]
        weights = w_all
    else:
        weights = w_ref
    tok_all[z] = tok_ref[...]
    gh_all[z] = gh_ref[z]
    gate_all[z] = gate_ref[z]
    err_copy.wait()

    def err_factor(c):
        cols = pl.ds(pl.multiple_of(c * chunk, chunk), chunk)
        facc[:, cols] = lax.dot_general(
            qt_ref[...], err_v[cols, :].astype(F32), (((1,), (1,)), ((), ())), precision=HI,
            preferred_element_type=F32)
    loop(width // chunk, err_factor, 0)
    each("expert", E, gate_copy, "recv")
    forward(1, "relay")
    if gather_w:
        each("dp", N, w_copy, "recv")

    def back_copy(d):
        dirn = jnp.where(d > z, 1, -1)
        direct = (d - z) * dirn == E - 1
        slot = jnp.where(direct, E + 1, jnp.where((d == z - 1), E, d))
        return rdma(back.at[d], ret.at[slot], b_s.at[d], b_r.at[slot], "expert",
                    jnp.where(direct, d, z + dirn))

    def back_wait(slot):
        rdma(back.at[0], ret.at[slot], b_s.at[0], b_r.at[slot], "expert",
             other("expert", E, 1)).wait_recv()

    def first_right(d):
        return jnp.where(d == E - 1, 1, 0)

    def first_left(d):
        return jnp.where(d == 0, E - 2, E - 1)

    def add_back(d, slot):
        back[d] = (back[d].astype(F32) + ret[slot].astype(F32)).astype(BF16)

    def block(i, c):
        s = i // 2
        d = lax.rem(i, 2)

        @pl.when((d == 0) & (s >= 2))
        def _():
            forward(s, "relay")

        j = z - (1 - 2 * d) * s

        @pl.when((j >= 0) & (j < E) & (i != 1))
        def _():
            @pl.when(s > 0)
            def _():
                gh_copy(j, j, 0).wait_recv()
            g = jnp.transpose(gate_all[j])[:, :1]
            x = (tok_all[j].astype(F32) * g).astype(BF16)
            x_all[j] = x
            pre = jnp.dot(x, weights[...], preferred_element_type=F32)
            gp = (gh_all[j].astype(F32) * slopes(pre)).astype(BF16)
            gp_all[j] = gp
            seen = lax.dot_general(gp.astype(F32), qt_ref[...], (((1,), (1,)), ((), ())),
                                   precision=HI, preferred_element_type=F32)
            facc[...] += lax.dot_general(seen, x.astype(F32), (((0,), (0,)), ((), ())),
                                         precision=HI, preferred_element_type=F32)
            rows = lax.dot_general(gp, weights[...], (((1,), (1,)), ((), ())),
                                   preferred_element_type=F32)
            back[j] = (rows * g).astype(BF16)

            @pl.when(((j > z) & (z <= first_right(j))) | ((j < z) & (z >= first_left(j))))
            def _():
                back_copy(j).start()
        return c
    lax.fori_loop(0, 2 * E, block, 0)

    if fbuf.shape[0] > groups * rank:
        fbuf[...] = jnp.zeros_like(fbuf)
    for c in range(groups):
        fbuf[c * rank : (c + 1) * rank, :] = facc[:, c * 128 : (c + 1) * 128]

    def f_copy(p, slot, k):
        return rdma(fbuf.at[pl.ds(pl.multiple_of(p * rp, 8), rp)], rsbuf.at[slot],
                    f_s.at[k], f_r.at[slot], "dp", p)

    def a_copy(p, slot, k):
        part = agbuf.at[pl.ds(pl.multiple_of(slot * rp, 8), rp)]
        return rdma(part, part, a_s.at[k], a_r.at[slot], "dp", p)

    def t_copy(p, slot, k):
        return rdma(tbuf.at[slot], tbuf.at[slot], t_s.at[k], t_r.at[slot], "dp", p)

    own = pl.ds(pl.multiple_of(me * rp, 8), rp)
    each("dp", N, f_copy, "start")
    rsbuf[me] = fbuf[own, :]
    def relay_right(d):
        @pl.when((d > z) & (z > first_right(d)))
        def _():
            back_wait(d)
            add_back(d, d)
            back_copy(d).start()
    loop(E, relay_right, 0)

    def relay_left(d):
        @pl.when((d < z) & (z < first_left(d)))
        def _():
            back_wait(d)
            add_back(d, d)
            back_copy(d).start()
    loop(E, relay_left, 0)

    def merge(c):
        cols = pl.ds(pl.multiple_of(c * chunk, chunk), chunk)
        x = x_all[:, :, cols].reshape(E * tokens, chunk)
        gp = gp_all[...].reshape(E * tokens, gp_all.shape[2])
        m = lax.dot_general(x, gp, (((0,), (0,)), ((), ())), preferred_element_type=F32)
        m = m + err_v[cols, :].astype(F32)
        merged[cols, :] = m
    loop(width // chunk, merge, 0)

    each("dp", N, f_copy, "recv")
    agbuf[own, :] = jnp.sum(rsbuf[...], axis=0) * (1.0 / N)
    each("dp", N, a_copy, "start")
    each("dp", N, a_copy, "recv")
    factor = jnp.concatenate([agbuf[c * rank : (c + 1) * rank, :] for c in range(groups)], axis=1)
    gram = lax.dot_general(factor, factor, (((1,), (1,)), ((), ())), precision=HI,
                           preferred_element_type=F32)
    basis = jnp.dot(inverse_factor(gram), factor, precision=HI, preferred_element_type=F32)
    right = jnp.dot(basis.astype(BF16), merged[...].astype(BF16), preferred_element_type=F32)
    tbuf[me] = right.astype(BF16)
    each("dp", N, t_copy, "start")
    basis_t = jnp.transpose(basis).astype(BF16)
    each("dp", N, t_copy, "recv")
    q_factor = (jnp.sum(tbuf[...].astype(F32), axis=0) * (1.0 / N)).astype(BF16)

    for c in range(width // chunk):
        cols = pl.ds(c * chunk, chunk)
        low = jnp.dot(basis_t[c * chunk : (c + 1) * chunk, :], q_factor,
                      preferred_element_type=F32)
        err_out[0, 0, cols, :] = (merged[cols, :] - low).astype(BF16)
        merged[cols, :] = low
    wg_out[0] = merged[pl.ds(pl.multiple_of(me * shard, 8), shard), :]

    @pl.when(z > first_right(z))
    def _():
        back_wait(z)
        add_back(z, z)

    @pl.when(z < first_left(z))
    def _():
        back_wait(E)
        add_back(z, E)

    @pl.when((z == 0) | (z == E - 1))
    def _():
        back_wait(E + 1)
        add_back(z, E + 1)
    gt_out[...] = back[z]

    forward_first = [(0, 1), (1, -1)]
    for d, dirn in forward_first:
        nb = z + dirn

        @pl.when((nb >= 0) & (nb < E))
        def _():
            rdma(tok_ref, tok_all.at[z], tok_s.at[d * E], tok_r.at[z], "expert", nb).wait_send()
    loop(E, lambda s: forward(s, "drain"))
    each("expert", E, gate_copy, "send")
    each("expert", E, gh_copy, "send")
    if gather_w:
        each("dp", N, w_copy, "send")
    loop(E, lambda k: back_copy(other("expert", E, k)).wait_send())
    each("dp", N, f_copy, "send")
    each("dp", N, a_copy, "send")
    each("dp", N, t_copy, "send")


def body(tokens, routes, gates, grad_hidden, w_in, error, q_seed):
    E = lax.axis_size("expert")
    N = lax.axis_size("dp")
    rows, width = tokens.shape
    hidden = grad_hidden.shape[2]
    rank = q_seed.shape[2]
    shard = width // N
    ids = jnp.arange(E, dtype=jnp.int32)
    hit0 = routes[None, :, 0] == ids[:, None]
    hit1 = routes[None, :, 1] == ids[:, None]
    gate_sel = jnp.where(hit0, gates[None, :, 0], jnp.where(hit1, gates[None, :, 1], 0.0))
    gate_sel = jnp.broadcast_to(gate_sel[:, None, :], (E, 8, rows))
    zero = jnp.zeros((), BF16)
    gh_sel = jnp.where(hit0[:, :, None], grad_hidden[None, :, 0, :],
                       jnp.where(hit1[:, :, None], grad_hidden[None, :, 1, :], zero))
    gather_w = shard % 16 == 0
    weight = w_in[0] if gather_w else lax.all_gather(w_in[0], "dp", axis=0, tiled=True)
    chunk = 256 if width % 256 == 0 else 128
    total_rows = width // 128 * rank
    rp = -(-total_rows // N)
    rp = -(-rp // 8) * 8
    room = (4 * E + 3) * rows * width * 2 + 3 * E * rows * hidden * 2 + 13 * width * hidden + (12 << 20)
    dma = pltpu.SemaphoreType.DMA
    vmem = pl.BlockSpec(memory_space=pltpu.VMEM)
    return pl.pallas_call(
        functools.partial(kernel, (E, N, rp, chunk, gather_w)),
        out_shape=(
            jax.ShapeDtypeStruct((rows, width), BF16),
            jax.ShapeDtypeStruct((1, 1, width, hidden), BF16),
            jax.ShapeDtypeStruct((1, shard, hidden), F32),
        ),
        in_specs=[vmem, vmem, vmem, vmem, pl.BlockSpec(memory_space=pl.ANY), vmem],
        out_specs=(vmem, vmem, vmem),
        scratch_shapes=[
            pltpu.VMEM((E, rows, width), BF16),
            pltpu.VMEM((E, rows, hidden), BF16),
            pltpu.VMEM((E, 8, rows), F32),
            pltpu.VMEM((width if gather_w else 16, hidden), BF16),
            pltpu.VMEM((E, rows, width), BF16),
            pltpu.VMEM((E, rows, hidden), BF16),
            pltpu.VMEM((width, hidden), BF16),
            pltpu.VMEM((width, hidden), F32),
            pltpu.VMEM((E, rows, width), BF16),
            pltpu.VMEM((E + 2, rows, width), BF16),
            pltpu.VMEM((rank, width), F32),
            pltpu.VMEM((rp * N, 128), F32),
            pltpu.VMEM((N, rp, 128), F32),
            pltpu.VMEM((rp * N, 128), F32),
            pltpu.VMEM((N, rank, hidden), BF16),
            dma(()), dma((2 * E,)), dma((E,)), dma((E,)), dma((E,)), dma((E,)), dma((E,)),
            dma((N,)), dma((N,)), dma((N,)), dma((N,)), dma((N,)), dma((N,)), dma((N,)), dma((N,)),
            dma((E,)), dma((E + 2,)),
        ],
        compiler_params=pltpu.CompilerParams(
            collective_id=0, has_side_effects=True, vmem_limit_bytes=min(room, 67043328 - (1 << 20))),
    )(tokens, gh_sel, gate_sel, weight, error, q_seed[0].T)


def solution(mesh):
    placed = (
        P(("dp", "expert"), None),
        P(("dp", "expert"), None),
        P(("dp", "expert"), None),
        P(("dp", "expert"), None, None),
        P("expert", "dp", None),
        P("dp", "expert", None, None),
        P("expert", None, None),
    )
    return jax.shard_map(
        body,
        mesh=mesh,
        in_specs=placed,
        out_specs=(
            P(("dp", "expert"), None),
            P("dp", "expert", None, None),
            P("expert", "dp", None),
        ),
        check_vma=False,
    )
```

profile of v0, /device:TPU:0, one launch (start us, length us, event | category | flops | bytes accessed | tf_op | source)
XLA Modules:
  0.0 80.5 jit_solution(1865817217273529673)
XLA Ops:
  0.6 0.0 copy-start.3
  0.6 0.0 copy-start
  0.7 0.0 copy-start.2
  0.7 0.0 copy-start.1
  0.7 0.8 %slice_bitcast_fusion.3 = (s32[128]{0:T(128)S(1)}, s32[128]{0:T(128)S(1)}) fusion(s32[128,2]{0,1:T(2,128)} %param.8), kind=kLoop, calls=%fused_computation.9 | loop fusion | bytes 2048 | tf_op jit(solution)/shard_map/eq | solution.py:317
  1.5 0.8 slice_bitcast_fusion.1
  2.3 1.5 %fusion = (bf16[128,1,512]{2,1,0:T(2,128)(2,1)S(1)}, bf16[128,1,512]{2,1,0:T(2,128)(2,1)S(1)}) fusion(bf16[128,2,512]{2,1,0:T(2,128)(2,1)} %param.10), kind=kLoop, calls=%fused_computation.10 | loop fusion | bytes 524288 | tf_op jit(solution)/shard_map/slice | solution.py:322
  3.8 0.2 select_select_fusion.gh_ref
  4.1 0.0 copy-done.3
  4.1 0.0 copy-done
  4.1 0.0 copy-done.2
  4.1 0.0 copy-done.1
  4.1 73.7 %shard_map.94 = (bf16[128,1792]{1,0:T(8,128)(2,1)S(1)}, bf16[1,1,1792,512]{3,2,1,0:T(8,128)(2,1)S(1)}, f32[1,224,512]{2,1,0:T(8,128)S(1)}) custom-call(bf16[128,1792]{1,0:T(8,128)(2,1)S(1)} %copy-done.1, bf16[4,128,512]{2,1,0:T(8,128)(2,1)S(1)} %select_select_fusion.gh_ref, f32[4,8,128]{2,1,0:T(8,128)S(1)} %broadcast_in_dim.86.gate_ref, ...), custom_call_target="tpu_custom_call" | custom-call | tf_op jit(solution)/shard_map/pallas_call | solution.py:333
  77.8 0.8 copy.19
  78.5 1.2 %copy.20 = bf16[1,1,1792,512]{3,2,1,0:T(8,128)(2,1)} copy(bf16[1,1,1792,512]{3,2,1,0:T(8,128)(2,1)S(1)} %get-tuple-element.17) | data formatting | bytes 3670016
  79.8 0.8 copy.21
  (4 shorter events, 0.1 us)
Async XLA Ops:
  0.6 3.4 %copy-start.3 = (f32[1,512,32]{1,2,0:T(8,128)S(1)}, f32[1,512,32]{1,2,0:T(8,128)}, u32[]{:S(2)}) copy-start(f32[1,512,32]{1,2,0:T(8,128)} %param.13) | copy-start | bytes 196612
  0.6 3.4 %copy-start = (bf16[1,1,1792,512]{3,2,1,0:T(8,128)(2,1)S(1)}, bf16[1,1,1792,512]{3,2,1,0:T(8,128)(2,1)}, u32[]{:S(2)}) copy-start(bf16[1,1,1792,512]{3,2,1,0:T(8,128)(2,1)} %err_hbm.1) | copy-start | bytes 5505028
  0.7 3.4 %copy-start.2 = (bf16[1,224,512]{2,1,0:T(8,128)(2,1)S(1)}, bf16[1,224,512]{2,1,0:T(8,128)(2,1)}, u32[]{:S(2)}) copy-start(bf16[1,224,512]{2,1,0:T(8,128)(2,1)} %param.11) | copy-start | bytes 688132
  0.7 3.4 %copy-start.1 = (bf16[128,1792]{1,0:T(8,128)(2,1)S(1)}, bf16[128,1792]{1,0:T(8,128)(2,1)}, u32[]{:S(2)}) copy-start(bf16[128,1792]{1,0:T(8,128)(2,1)} %tok_ref.1) | copy-start | bytes 1376260
where the time goes:
time: 80.7 us; the launch traced here: 80.5 us
  Pallas kernels  73.7 us (91%)
  local copies, waits for them, and re-layouts  5.93 us (7%)
    pallas_call x1, Pallas kernels, body(): pl.pallas_call(functools.partial(kernel, (E, N, rp, chunk, gather_w)), ou...  73.7 us
    unnamed x11, local copies, waits for them, and re-layouts  2.78 us

commit v1 on v0

v1 whole, which is shorter than its diff:
```python
import functools

import jax
import jax.numpy as jnp
from jax import lax
from jax.experimental import pallas as pl
from jax.experimental.pallas import tpu as pltpu
from jax.sharding import PartitionSpec as P

HI = lax.Precision.HIGHEST
MESH = pl.DeviceIdType.MESH
F32 = jnp.float32
BF16 = jnp.bfloat16
NT = (((1,), (1,)), ((), ()))
TN = (((0,), (0,)), ((), ()))


def slopes(pre_act):
    squashed = 1.0 / (1.0 + jnp.exp(-pre_act))
    return squashed * (1.0 + pre_act * (1.0 - squashed))


def halves(value):
    high = value.astype(BF16)
    low = (value - high.astype(F32)).astype(BF16)
    return jnp.concatenate([high, low], axis=0)


def fold(value):
    rows = value.shape[0] // 2
    return value[:rows] + value[rows:]


def inverse_factor(gram):
    rank = gram.shape[0]
    rows = lax.broadcasted_iota(jnp.int32, (rank, rank), 0)
    cols = lax.broadcasted_iota(jnp.int32, (rank, rank), 1)
    left = gram
    right = (rows == cols).astype(F32)
    row_id = lax.broadcasted_iota(jnp.int32, (rank, 1), 0)
    for i in range(rank - 1):
        scale = 1.0 / left[i : i + 1, i : i + 1]
        col = jnp.where(row_id > i, left[:, i : i + 1], 0.0)
        row_l = left[i : i + 1, :] * scale
        row_r = right[i : i + 1, :] * scale
        left = left - col * row_l
        right = right - col * row_r
    pivots = jnp.sum(jnp.where(rows == cols, left, 0.0), axis=1, keepdims=True)
    return right * (1.0 / jnp.sqrt(pivots))


def kernel(dims, tok_hbm, gh_hbm, rt_hbm, gt_hbm, w_hbm, err_hbm, q_hbm,
           gt_out, err_out, wg_out,
           tok_all, gh_raw, gh_sel, gh_all, rt_v, gt_v, gate_sel, gate_all, w_all, x_all, gp_all,
           err_v, merged, merged_b, back, ret, q_v, q2, facc, fbuf, rsbuf, agbuf, tbuf, bt_v,
           in_s, tok_s, tok_r, gh_s, gh_r, gate_s, gate_r, w_s, w_r,
           f_s, f_r, a_s, a_r, t_s, t_r, b_s, b_r):
    E, N, rp, chunk, gather_w, C = dims
    z = lax.axis_index("expert")
    me = lax.axis_index("dp")
    tokens, width = tok_hbm.shape
    shard = width // N
    rank = q_hbm.shape[0]
    groups = width // 128
    part = tokens // C
    ready = C

    def other(axis, size, k):
        return lax.rem(lax.axis_index(axis) + k, size)

    def loop(size, fn, start=1):
        def step(k, c):
            fn(k)
            return c
        lax.fori_loop(start, size, step, 0)

    barrier = pltpu.get_barrier_semaphore()
    loop(E, lambda k: pl.semaphore_signal(
        barrier, inc=1, device_id={"expert": other("expert", E, k)}, device_id_type=MESH))
    loop(N, lambda k: pl.semaphore_signal(
        barrier, inc=1, device_id={"dp": other("dp", N, k)}, device_id_type=MESH))

    def w_rows(slot):
        return w_all.at[pl.ds(pl.multiple_of(slot * shard, 16), shard)] if gather_w else w_all

    loads = [
        pltpu.make_async_copy(tok_hbm, tok_all.at[z], in_s.at[0]),
        pltpu.make_async_copy(w_hbm, w_rows(me), in_s.at[1]),
        pltpu.make_async_copy(rt_hbm, rt_v, in_s.at[2]),
        pltpu.make_async_copy(gt_hbm, gt_v, in_s.at[3]),
        pltpu.make_async_copy(gh_hbm, gh_raw, in_s.at[4]),
        pltpu.make_async_copy(q_hbm, q_v, in_s.at[5]),
        pltpu.make_async_copy(err_hbm.at[0, 0], err_v, in_s.at[6]),
    ]
    for load in loads:
        load.start()

    def rdma(src, dst, s, r, axis, peer):
        return pltpu.make_async_remote_copy(
            src_ref=src, dst_ref=dst, send_sem=s, recv_sem=r,
            device_id={axis: peer}, device_id_type=MESH)

    def gate_copy(p, slot, k):
        return rdma(gate_sel.at[p], gate_all.at[slot], gate_s.at[k], gate_r.at[slot], "expert", p)

    def gh_copy(p, slot, k):
        return rdma(gh_sel.at[p], gh_all.at[slot], gh_s.at[k], gh_r.at[slot], "expert", p)

    def rows_of(c):
        return pl.ds(pl.multiple_of(c * part, 16), part)

    def tok_copy(j, c, nb, d):
        piece = tok_all.at[j, rows_of(c)]
        return rdma(piece, piece, tok_s.at[d, j, c], tok_r.at[j, c], "expert", nb)

    def w_copy(p, slot, k):
        return rdma(w_rows(slot), w_rows(slot), w_s.at[k], w_r.at[slot], "dp", p)

    def each(p_axis, size, copy, act):
        mine = lax.axis_index(p_axis)

        def fn(k):
            p = other(p_axis, size, k)
            if act == "start":
                copy(p, mine, k).start()
            elif act == "recv":
                copy(p, p, k).wait_recv()
            else:
                copy(p, mine, k).wait_send()
        loop(size, fn)

    partner = me + 1 - 2 * lax.rem(me, 2)
    half = N // 2

    def cross(k):
        return me + 2 * (lax.bitwise_xor(me // 2, k) - me // 2)

    for i in range(4):
        loads[i].wait()
    pl.semaphore_wait(barrier, E - 1 + N - 1)

    for d, dirn in enumerate((1, -1)):
        nb = z + dirn
        ahead = z if d == 0 else E - 1 - z

        @pl.when((nb >= 0) & (nb < E))
        def _():
            tok_copy(z, 0, nb, d).start()

            @pl.when(ahead == 0)
            def _():
                loop(C, lambda c: tok_copy(z, c, nb, d).start())
    if gather_w:
        loop(half, lambda k: w_copy(cross(k), me, k).start())
        w_copy(partner, me, 0).start()

    routes = rt_v[...]
    gates = gt_v[...]

    def pick_gate(e):
        row = jnp.where(routes[0:1] == e, gates[0:1], jnp.where(routes[1:2] == e, gates[1:2], 0.0))
        gate_sel[e] = jnp.broadcast_to(row, (8, tokens))
    loop(E, pick_gate, 0)
    each("expert", E, gate_copy, "start")
    gate_all[z] = gate_sel[z]

    loads[4].wait()
    pairs = gh_raw[...].reshape(2 * tokens, gh_raw.shape[2])
    named = jnp.transpose(jnp.concatenate([routes.astype(F32)] * 4, axis=0))
    t_id = lax.broadcasted_iota(jnp.int32, (tokens, 2 * tokens), 0)
    p_id = lax.broadcasted_iota(jnp.int32, (tokens, 2 * tokens), 1)
    wanted = jnp.where(p_id == 2 * t_id, named[:, 0:1],
                       jnp.where(p_id == 2 * t_id + 1, named[:, 1:2], -1.0))

    def pick_rows(e):
        choose = jnp.where(wanted == e.astype(F32), 1.0, 0.0).astype(BF16)
        gh_sel[e] = jnp.dot(choose, pairs, preferred_element_type=F32).astype(BF16)

    def send_rows(k):
        p = other("expert", E, k)
        pick_rows(p)
        gh_copy(p, z, k).start()
    loop(E, send_rows)
    pick_rows(z)
    gh_all[z] = gh_sel[z]

    loads[5].wait()
    loads[6].wait()
    q2[...] = halves(q_v[...])

    def err_factor(c):
        cols = pl.ds(pl.multiple_of(c * chunk, chunk), chunk)
        facc[:, cols] = fold(lax.dot_general(
            q2[...], err_v[cols, :], NT, preferred_element_type=F32))
    loop(width // chunk, err_factor, 0)

    def back_copy(dest, c):
        dirn = jnp.where(dest > z, 1, -1)
        nb = z + dirn
        slot = jnp.where((dest == nb) & (dest < z), E, dest)
        return rdma(back.at[dest, rows_of(c)], ret.at[slot, rows_of(c)],
                    b_s.at[dest, c], b_r.at[slot, c], "expert", nb)

    def back_wait(slot, c):
        rdma(back.at[0, rows_of(c)], ret.at[slot, rows_of(c)], b_s.at[0, c], b_r.at[slot, c],
             "expert", other("expert", E, 1)).wait_recv()

    def add_back(dest, slot, c):
        rows = rows_of(c)
        back[dest, rows, :] = (back[dest, rows, :].astype(F32)
                               + ret[slot, rows, :].astype(F32)).astype(BF16)

    def compute(j):
        @pl.when(j != z)
        def _():
            gate_copy(j, j, 0).wait_recv()
            gh_copy(j, j, 0).wait_recv()
        g = jnp.transpose(gate_all[j])[:, :1]
        x = (tok_all[j].astype(F32) * g).astype(BF16)
        x_all[j] = x
        pre = jnp.dot(x, w_all[...], preferred_element_type=F32)
        gp = (gh_all[j].astype(F32) * slopes(pre)).astype(BF16)
        gp_all[j] = gp
        seen = fold(lax.dot_general(q2[...], gp, NT, preferred_element_type=F32))
        facc[...] += fold(jnp.dot(halves(seen), x, preferred_element_type=F32))
        back[j] = (lax.dot_general(gp, w_all[...], NT, preferred_element_type=F32) * g).astype(BF16)

        @pl.when(((j > z) & (z == 0)) | ((j < z) & (z == E - 1)))
        def _():
            loop(C, lambda c: back_copy(j, c).start(), 0)

    def stage(e, ahead):
        early = e < ahead
        rest = jnp.maximum(e - ahead, 0)
        s = jnp.where(early, e + 1, ahead - rest // (C - 1))
        c = jnp.where(early, 0, lax.rem(rest, C - 1) + 1)
        return s, c, e < ahead * C

    def event(e):
        for d, dirn in enumerate((1, -1)):
            ahead = z if d == 0 else E - 1 - z
            s, c, valid = stage(e, ahead)
            j = z - dirn * s
            nb = z + dirn
            linked = (nb >= 0) & (nb < E)

            @pl.when(valid)
            def _():
                tok_copy(j, c, z, d).wait_recv()

                @pl.when(linked)
                def _():
                    tok_copy(j, c, nb, d).start()

                    @pl.when(e == ahead * C - 1)
                    def _():
                        loop(C, lambda k: tok_copy(z, k, nb, d).start())
        if gather_w:
            @pl.when(e == 2)
            def _():
                def forward(k):
                    w_copy(cross(k), cross(k), 0).wait_recv()
                    w_copy(partner, cross(k), half + k).start()
                loop(min(3, half), forward)

            @pl.when(e == ready)
            def _():
                def forward(k):
                    w_copy(cross(k), cross(k), 0).wait_recv()
                    w_copy(partner, cross(k), half + k).start()
                loop(half, forward, min(3, half))
                w_copy(partner, partner, 0).wait_recv()
                loop(half, lambda k: w_copy(partner, partner + cross(k) - me, 0).wait_recv())

        def slot(i, carry):
            ahead = jnp.where(i == 0, z, E - 1 - z)
            dirn = 1 - 2 * i
            s, c, valid = stage(e, ahead)
            first = ahead + C - 2
            late = (e == ready) & (first < ready) & (ahead > 0)
            done = (e >= ready) & valid & (c == C - 1)
            own = (i == 2) & (e == ready + 2)
            j = jnp.where(own, z, jnp.where(late, z - dirn * ahead, z - dirn * s))

            @pl.when(own | ((i < 2) & (late | done)))
            def _():
                compute(j)
            return carry

        @pl.when(e >= ready)
        def _():
            lax.fori_loop(0, 3, slot, 0)
    loop((E - 1) * C, event, 0)

    if fbuf.shape[0] > groups * rank:
        fbuf[...] = jnp.zeros_like(fbuf)
    for c in range(groups):
        fbuf[c * rank : (c + 1) * rank, :] = facc[:, c * 128 : (c + 1) * 128]

    def f_copy(p, slot, k):
        return rdma(fbuf.at[pl.ds(pl.multiple_of(p * rp, 8), rp)], rsbuf.at[slot],
                    f_s.at[k], f_r.at[slot], "dp", p)

    def a_copy(p, slot, k):
        piece = agbuf.at[pl.ds(pl.multiple_of(slot * rp, 8), rp)]
        return rdma(piece, piece, a_s.at[k], a_r.at[slot], "dp", p)

    def t_copy(p, slot, k):
        return rdma(tbuf.at[slot], tbuf.at[slot], t_s.at[k], t_r.at[slot], "dp", p)

    own = pl.ds(pl.multiple_of(me * rp, 8), rp)
    each("dp", N, f_copy, "start")
    rsbuf[me] = fbuf[own, :]

    def merge(c):
        cols = pl.ds(pl.multiple_of(c * chunk, chunk), chunk)
        x = x_all[:, :, cols].reshape(E * tokens, chunk)
        gp = gp_all[...].reshape(E * tokens, gp_all.shape[2])
        m = lax.dot_general(x, gp, TN, preferred_element_type=F32)
        m = m + err_v[cols, :].astype(F32)
        merged[cols, :] = m
        merged_b[cols, :] = m.astype(BF16)
    loop(width // chunk, merge, 0)

    each("dp", N, f_copy, "recv")
    agbuf[own, :] = jnp.sum(rsbuf[...], axis=0) * (1.0 / N)
    each("dp", N, a_copy, "start")

    right_first = z < E - 1 - z

    def relay(dest):
        def piece(c):
            back_wait(dest, c)
            add_back(dest, dest, c)
            back_copy(dest, c).start()
        loop(C, piece, 0)

    def relay_right(k):
        dest = E - k

        @pl.when((dest > z) & (z > 0))
        def _():
            relay(dest)

    def relay_left(k):
        dest = k - 1

        @pl.when((dest < z) & (z < E - 1))
        def _():
            relay(dest)

    @pl.when(right_first)
    def _():
        loop(E, relay_right)

    @pl.when(jnp.logical_not(right_first))
    def _():
        loop(E, relay_left)

    each("dp", N, a_copy, "recv")
    factor = jnp.concatenate([agbuf[c * rank : (c + 1) * rank, :] for c in range(groups)], axis=1)
    tbuf[me] = fold(jnp.dot(halves(factor), merged_b[...], preferred_element_type=F32)).astype(BF16)
    each("dp", N, t_copy, "start")

    gram = lax.dot_general(factor, factor, NT, precision=HI, preferred_element_type=F32)
    inverse = inverse_factor(gram)
    basis = jnp.dot(inverse, factor, precision=HI, preferred_element_type=F32)
    bt_v[...] = jnp.transpose(basis).astype(BF16)

    @pl.when(right_first)
    def _():
        loop(E, relay_left)

    @pl.when(jnp.logical_not(right_first))
    def _():
        loop(E, relay_right)

    each("dp", N, t_copy, "recv")
    mean = jnp.sum(tbuf[...].astype(F32), axis=0) * (1.0 / N)
    q_factor = jnp.dot(inverse, mean, precision=HI, preferred_element_type=F32).astype(BF16)

    for c in range(width // chunk):
        cols = pl.ds(c * chunk, chunk)
        low = jnp.dot(bt_v[cols, :], q_factor, preferred_element_type=F32)
        err_out[0, 0, cols, :] = (merged[cols, :] - low).astype(BF16)
    wg_out[0] = jnp.dot(bt_v[pl.ds(pl.multiple_of(me * shard, 8), shard), :], q_factor,
                        preferred_element_type=F32)

    @pl.when(z > 0)
    def _():
        def piece(c):
            back_wait(z, c)
            add_back(z, z, c)
        loop(C, piece, 0)

    @pl.when(z < E - 1)
    def _():
        def piece(c):
            back_wait(E, c)
            add_back(z, E, c)
        loop(C, piece, 0)
    gt_out[...] = back[z]

    for d, dirn in enumerate((1, -1)):
        nb = z + dirn
        ahead = z if d == 0 else E - 1 - z

        @pl.when((nb >= 0) & (nb < E))
        def _():
            def drain(s):
                @pl.when(s <= ahead)
                def _():
                    loop(C, lambda c: tok_copy(z - dirn * s, c, nb, d).wait_send(), 0)
            loop(E, drain, 0)
    each("expert", E, gate_copy, "send")
    each("expert", E, gh_copy, "send")
    if gather_w:
        loop(half, lambda k: w_copy(cross(k), me, k).wait_send())
        w_copy(partner, me, 0).wait_send()
        loop(half, lambda k: w_copy(partner, cross(k), half + k).wait_send())

    def sent(k):
        dest = other("expert", E, k)
        loop(C, lambda c: back_copy(dest, c).wait_send(), 0)
    loop(E, sent)
    each("dp", N, f_copy, "send")
    each("dp", N, a_copy, "send")
    each("dp", N, t_copy, "send")


def body(tokens, routes, gates, grad_hidden, w_in, error, q_seed):
    E = lax.axis_size("expert")
    N = lax.axis_size("dp")
    rows, width = tokens.shape
    hidden = grad_hidden.shape[2]
    rank = q_seed.shape[2]
    shard = width // N
    gather_w = shard % 16 == 0 and N & (N - 1) == 0
    weight = w_in[0] if gather_w else lax.all_gather(w_in[0], "dp", axis=0, tiled=True)
    chunk = 256 if width % 256 == 0 else 128
    C = 4 if E <= 8 else 2
    total_rows = width // 128 * rank
    rp = -(-total_rows // N)
    rp = -(-rp // 8) * 8
    dma = pltpu.SemaphoreType.DMA
    vmem = pl.BlockSpec(memory_space=pltpu.VMEM)
    hbm = pl.BlockSpec(memory_space=pltpu.HBM)
    return pl.pallas_call(
        functools.partial(kernel, (E, N, rp, chunk, gather_w, C)),
        out_shape=(
            jax.ShapeDtypeStruct((rows, width), BF16),
            jax.ShapeDtypeStruct((1, 1, width, hidden), BF16),
            jax.ShapeDtypeStruct((1, shard, hidden), F32),
        ),
        in_specs=[hbm] * 7,
        out_specs=(vmem, vmem, vmem),
        scratch_shapes=[
            pltpu.VMEM((E, rows, width), BF16),
            pltpu.VMEM((rows, 2, hidden), BF16),
            pltpu.VMEM((E, rows, hidden), BF16),
            pltpu.VMEM((E, rows, hidden), BF16),
            pltpu.VMEM((2, rows), jnp.int32),
            pltpu.VMEM((2, rows), F32),
            pltpu.VMEM((E, 8, rows), F32),
            pltpu.VMEM((E, 8, rows), F32),
            pltpu.VMEM((width, hidden), BF16),
            pltpu.VMEM((E, rows, width), BF16),
            pltpu.VMEM((E, rows, hidden), BF16),
            pltpu.VMEM((width, hidden), BF16),
            pltpu.VMEM((width, hidden), F32),
            pltpu.VMEM((width, hidden), BF16),
            pltpu.VMEM((E, rows, width), BF16),
            pltpu.VMEM((E + 1, rows, width), BF16),
            pltpu.VMEM((rank, hidden), F32),
            pltpu.VMEM((2 * rank, hidden), BF16),
            pltpu.VMEM((rank, width), F32),
            pltpu.VMEM((rp * N, 128), F32),
            pltpu.VMEM((N, rp, 128), F32),
            pltpu.VMEM((rp * N, 128), F32),
            pltpu.VMEM((N, rank, hidden), BF16),
            pltpu.VMEM((width, rank), BF16),
            dma((7,)), dma((2, E, C)), dma((E, C)), dma((E,)), dma((E,)), dma((E,)), dma((E,)),
            dma((N,)), dma((N,)), dma((N,)), dma((N,)), dma((N,)), dma((N,)), dma((N,)), dma((N,)),
            dma((E, C)), dma((E + 1, C)),
        ],
        compiler_params=pltpu.CompilerParams(
            collective_id=0, has_side_effects=True, vmem_limit_bytes=67043328 - (1 << 20)),
    )(tokens, grad_hidden, routes.T, gates.T, weight, error, q_seed[0].T)


def solution(mesh):
    placed = (
        P(("dp", "expert"), None),
        P(("dp", "expert"), None),
        P(("dp", "expert"), None),
        P(("dp", "expert"), None, None),
        P("expert", "dp", None),
        P("dp", "expert", None, None),
        P("expert", None, None),
    )
    return jax.shard_map(
        body,
        mesh=mesh,
        in_specs=placed,
        out_specs=(
            P(("dp", "expert"), None),
            P("dp", "expert", None, None),
            P("expert", "dp", None),
        ),
        check_vma=False,
    )
```

time: 80.7 us -> 84.9 us (1.052)
  Pallas kernels: 73.7 us -> 78.5 us
    pallas_call x1, Pallas kernels: 73.7 us -> 78.5 us  [body(): pl.pallas_call(functools.partial(kernel, (E, N, rp, chunk, gather_w, C)),...]
    unnamed x11 -> x5, local copies, waits for them, and re-layouts: 2.78 us -> 5.49 us
    slice x1 -> x0, local copies, waits for them, and re-layouts: 1.49 us -> none  [body(): grad_hidden[None, :, 0, :]]
    eq x1 -> x0, local copies, waits for them, and re-layouts: 0.85 us -> none  [body(): hit0 = routes[None, :, 0] == ids[:, None]]
where the time goes in v1:
time: 84.9 us; the launch traced here: 84.6 us
  Pallas kernels  78.5 us (92%)
  local copies, waits for them, and re-layouts  5.49 us (6%)
    pallas_call x1, Pallas kernels, body(): pl.pallas_call(functools.partial(kernel, (E, N, rp, chunk, gather_w, C)),...  78.5 us
    unnamed x5, local copies, waits for them, and re-layouts  5.49 us

profile of v1, /device:TPU:0, one launch (start us, length us, event | category | flops | bytes accessed | tf_op | source)
XLA Modules:
  0.0 84.6 jit_solution(9835312914114829790)
XLA Ops:
  0.6 78.5 %shard_map.94 = (bf16[128,1792]{1,0:T(8,128)(2,1)}, bf16[1,1,1792,512]{3,2,1,0:T(8,128)(2,1)}, f32[1,224,512]{2,1,0:T(8,128)}) custom-call(bf16[128,1792]{1,0:T(8,128)(2,1)} %tok_hbm.1, bf16[128,2,512]{2,1,0:T(2,128)(2,1)} %gh_hbm.1, s32[2,128]{1,0:T(2,128)} %bitcast.8, f32[2,128]{1,0:T(2,128)} %bitcast.9, bf16[224,512]{1,0:T(8,128)(2,1)} %bitcast.6, ...), custom_call_target="tpu_custom_call" | custom-call | tf_op jit(solution)/shard_map/pallas_call | solution.py:448
  79.2 1.8 %copy.13 = bf16[128,1792]{1,0:T(8,128)(2,1)} copy(bf16[128,1792]{1,0:T(8,128)(2,1)} %get-tuple-element.6) | data formatting | bytes 917504
  81.0 0.0 copy-start
  81.0 2.9 %copy.14 = bf16[1,1,1792,512]{3,2,1,0:T(8,128)(2,1)} copy(bf16[1,1,1792,512]{3,2,1,0:T(8,128)(2,1)} %get-tuple-element.7) | data formatting | bytes 3670016
  83.9 0.0 copy-done
  83.9 0.8 copy.15
Async XLA Ops:
  81.0 2.9 %copy-start = (f32[1,224,512]{2,1,0:T(8,128)S(1)}, f32[1,224,512]{2,1,0:T(8,128)}, u32[]{:S(2)}) copy-start(f32[1,224,512]{2,1,0:T(8,128)} %get-tuple-element.8) | copy-start | bytes 1376260

commit v2 on v1

--- a/solution.py
+++ b/solution.py
@@ -55,7 +55,7 @@
            err_v, merged, merged_b, back, ret, q_v, q2, facc, fbuf, rsbuf, agbuf, tbuf, bt_v,
            in_s, tok_s, tok_r, gh_s, gh_r, gate_s, gate_r, w_s, w_r,
            f_s, f_r, a_s, a_r, t_s, t_r, b_s, b_r):
-    E, N, rp, chunk, gather_w, C = dims
+    E, N, rp, chunk, gather_w, C, CB = dims
     z = lax.axis_index("expert")
     me = lax.axis_index("dp")
     tokens, width = tok_hbm.shape
@@ -63,7 +63,7 @@
     rank = q_hbm.shape[0]
     groups = width // 128
     part = tokens // C
-    ready = C
+    back_part = tokens // CB
 
     def other(axis, size, k):
         return lax.rem(lax.axis_index(axis) + k, size)
@@ -141,15 +141,10 @@
 
     for d, dirn in enumerate((1, -1)):
         nb = z + dirn
-        ahead = z if d == 0 else E - 1 - z
 
         @pl.when((nb >= 0) & (nb < E))
         def _():
-            tok_copy(z, 0, nb, d).start()
-
-            @pl.when(ahead == 0)
-            def _():
-                loop(C, lambda c: tok_copy(z, c, nb, d).start())
+            loop(C, lambda c: tok_copy(z, c, nb, d).start(), 0)
     if gather_w:
         loop(half, lambda k: w_copy(cross(k), me, k).start())
         w_copy(partner, me, 0).start()
@@ -194,103 +189,94 @@
             q2[...], err_v[cols, :], NT, preferred_element_type=F32))
     loop(width // chunk, err_factor, 0)
 
+    def back_rows(c):
+        return pl.ds(pl.multiple_of(c * back_part, 16), back_part)
+
     def back_copy(dest, c):
         dirn = jnp.where(dest > z, 1, -1)
         nb = z + dirn
         slot = jnp.where((dest == nb) & (dest < z), E, dest)
-        return rdma(back.at[dest, rows_of(c)], ret.at[slot, rows_of(c)],
+        return rdma(back.at[dest, back_rows(c)], ret.at[slot, back_rows(c)],
                     b_s.at[dest, c], b_r.at[slot, c], "expert", nb)
 
     def back_wait(slot, c):
-        rdma(back.at[0, rows_of(c)], ret.at[slot, rows_of(c)], b_s.at[0, c], b_r.at[slot, c],
+        rdma(back.at[0, back_rows(c)], ret.at[slot, back_rows(c)], b_s.at[0, c], b_r.at[slot, c],
              "expert", other("expert", E, 1)).wait_recv()
 
     def add_back(dest, slot, c):
-        rows = rows_of(c)
+        rows = back_rows(c)
         back[dest, rows, :] = (back[dest, rows, :].astype(F32)
                                + ret[slot, rows, :].astype(F32)).astype(BF16)
 
-    def compute(j):
+    def gate_column(j):
+        return jnp.transpose(gate_all[j])[:, :1]
+
+    def inward(j):
         @pl.when(j != z)
         def _():
             gate_copy(j, j, 0).wait_recv()
             gh_copy(j, j, 0).wait_recv()
-        g = jnp.transpose(gate_all[j])[:, :1]
-        x = (tok_all[j].astype(F32) * g).astype(BF16)
+        x = (tok_all[j].astype(F32) * gate_column(j)).astype(BF16)
         x_all[j] = x
         pre = jnp.dot(x, w_all[...], preferred_element_type=F32)
         gp = (gh_all[j].astype(F32) * slopes(pre)).astype(BF16)
         gp_all[j] = gp
         seen = fold(lax.dot_general(q2[...], gp, NT, preferred_element_type=F32))
         facc[...] += fold(jnp.dot(halves(seen), x, preferred_element_type=F32))
-        back[j] = (lax.dot_general(gp, w_all[...], NT, preferred_element_type=F32) * g).astype(BF16)
+
+    def outward(j):
+        back[j] = (lax.dot_general(gp_all[j], w_all[...], NT, preferred_element_type=F32)
+                   * gate_column(j)).astype(BF16)
 
         @pl.when(((j > z) & (z == 0)) | ((j < z) & (z == E - 1)))
         def _():
-            loop(C, lambda c: back_copy(j, c).start(), 0)
-
-    def stage(e, ahead):
-        early = e < ahead
-        rest = jnp.maximum(e - ahead, 0)
-        s = jnp.where(early, e + 1, ahead - rest // (C - 1))
-        c = jnp.where(early, 0, lax.rem(rest, C - 1) + 1)
-        return s, c, e < ahead * C
-
-    def event(e):
-        for d, dirn in enumerate((1, -1)):
-            ahead = z if d == 0 else E - 1 - z
-            s, c, valid = stage(e, ahead)
-            j = z - dirn * s
-            nb = z + dirn
-            linked = (nb >= 0) & (nb < E)
-
-            @pl.when(valid)
+            loop(CB, lambda c: back_copy(j, c).start(), 0)
+
+    def forward(s):
+        def piece(c):
+            for d, dirn in enumerate((1, -1)):
+                j = z - dirn * s
+                nb = z + dirn
+
+                @pl.when((j >= 0) & (j < E))
+                def _():
+                    tok_copy(j, c, z, d).wait_recv()
+
+                    @pl.when((nb >= 0) & (nb < E))
+                    def _():
+                        tok_copy(j, c, nb, d).start()
+        loop(C, piece, 0)
+
+    def weights():
+        def pass_on(k):
+            w_copy(cross(k), cross(k), 0).wait_recv()
+            w_copy(partner, cross(k), half + k).start()
+        loop(half, pass_on)
+        w_copy(partner, partner, 0).wait_recv()
+        loop(half, lambda k: w_copy(partner, partner + cross(k) - me, 0).wait_recv())
+
+    farthest = jnp.maximum(z, E - 1 - z)
+
+    def step(s):
+        forward(s)
+        if gather_w:
+            @pl.when(s == 1)
             def _():
-                tok_copy(j, c, z, d).wait_recv()
-
-                @pl.when(linked)
+                weights()
+
+        def block(i, carry):
+            j = jnp.where(i == 0, z, jnp.where(i == 1, z - s, z + s))
+
+            @pl.when((j >= 0) & (j < E) & ((i > 0) | (s == 1)))
+            def _():
+                inward(j)
+
+                @pl.when((s < farthest) | (i == 0))
                 def _():
-                    tok_copy(j, c, nb, d).start()
-
-                    @pl.when(e == ahead * C - 1)
-                    def _():
-                        loop(C, lambda k: tok_copy(z, k, nb, d).start())
-        if gather_w:
-            @pl.when(e == 2)
-            def _():
-                def forward(k):
-                    w_copy(cross(k), cross(k), 0).wait_recv()
-                    w_copy(partner, cross(k), half + k).start()
-                loop(min(3, half), forward)
-
-            @pl.when(e == ready)
-            def _():
-                def forward(k):
-                    w_copy(cross(k), cross(k), 0).wait_recv()
-                    w_copy(partner, cross(k), half + k).start()
-                loop(half, forward, min(3, half))
-                w_copy(partner, partner, 0).wait_recv()
-                loop(half, lambda k: w_copy(partner, partner + cross(k) - me, 0).wait_recv())
-
-        def slot(i, carry):
-            ahead = jnp.where(i == 0, z, E - 1 - z)
-            dirn = 1 - 2 * i
-            s, c, valid = stage(e, ahead)
-            first = ahead + C - 2
-            late = (e == ready) & (first < ready) & (ahead > 0)
-            done = (e >= ready) & valid & (c == C - 1)
-            own = (i == 2) & (e == ready + 2)
-            j = jnp.where(own, z, jnp.where(late, z - dirn * ahead, z - dirn * s))
-
-            @pl.when(own | ((i < 2) & (late | done)))
-            def _():
-                compute(j)
+                    outward(j)
             return carry
-
-        @pl.when(e >= ready)
-        def _():
-            lax.fori_loop(0, 3, slot, 0)
-    loop((E - 1) * C, event, 0)
+        lax.fori_loop(0, 3, block, 0)
+    loop(E, step)
 
     if fbuf.shape[0] > groups * rank:
         fbuf[...] = jnp.zeros_like(fbuf)
@@ -311,6 +297,39 @@
     own = pl.ds(pl.multiple_of(me * rp, 8), rp)
     each("dp", N, f_copy, "start")
     rsbuf[me] = fbuf[own, :]
+
+    def last_block(i, carry):
+        j = jnp.where(i == 0, z - farthest, z + farthest)
+
+        @pl.when((j >= 0) & (j < E))
+        def _():
+            outward(j)
+        return carry
+    lax.fori_loop(0, 2, last_block, 0)
+
+    right_first = z < E - 1 - z
+    lag = 3
+
+    def relay(m, c):
+        def turn(i, carry):
+            right = (i == 0) == right_first
+            dest = jnp.where(right, m, E - 1 - m)
+            hop = jnp.where(right, (dest > z) & (z > 0), (dest < z) & (z < E - 1))
+            piece = c - lag * i
+
+            @pl.when(hop & (piece >= 0) & (piece < CB))
+            def _():
+                back_wait(dest, piece)
+                add_back(dest, dest, piece)
+                back_copy(dest, piece).start()
+            return carry
+        lax.fori_loop(0, 2, turn, 0)
+
+    def relays(start, stop, first, last):
+        def rank_of(m, carry):
+            loop(last, lambda c: relay(m, c), first)
+            return carry
+        lax.fori_loop(start, stop, rank_of, 0)
 
     def merge(c):
         cols = pl.ds(pl.multiple_of(c * chunk, chunk), chunk)
@@ -321,42 +340,12 @@
         merged[cols, :] = m
         merged_b[cols, :] = m.astype(BF16)
     loop(width // chunk, merge, 0)
-
+    relays(1, E - 1, 0, CB // 2)
     each("dp", N, f_copy, "recv")
     agbuf[own, :] = jnp.sum(rsbuf[...], axis=0) * (1.0 / N)
     each("dp", N, a_copy, "start")
 
-    right_first = z < E - 1 - z
-
-    def relay(dest):
-        def piece(c):
-            back_wait(dest, c)
-            add_back(dest, dest, c)
-            back_copy(dest, c).start()
-        loop(C, piece, 0)
-
-    def relay_right(k):
-        dest = E - k
-
-        @pl.when((dest > z) & (z > 0))
-        def _():
-            relay(dest)
-
-    def relay_left(k):
-        dest = k - 1
-
-        @pl.when((dest < z) & (z < E - 1))
-        def _():
-            relay(dest)
-
-    @pl.when(right_first)
-    def _():
-        loop(E, relay_right)
-
-    @pl.when(jnp.logical_not(right_first))
-    def _():
-        loop(E, relay_left)
-
+    relays(1, E - 1, CB // 2, CB + lag)
     each("dp", N, a_copy, "recv")
     factor = jnp.concatenate([agbuf[c * rank : (c + 1) * rank, :] for c in range(groups)], axis=1)
     tbuf[me] = fold(jnp.dot(halves(factor), merged_b[...], preferred_element_type=F32)).astype(BF16)
@@ -367,40 +356,7 @@
     basis = jnp.dot(inverse, factor, precision=HI, preferred_element_type=F32)
     bt_v[...] = jnp.transpose(basis).astype(BF16)
 
-    @pl.when(right_first)
-    def _():
-        loop(E, relay_left)
-
-    @pl.when(jnp.logical_not(right_first))
-    def _():
-        loop(E, relay_right)
-
-    each("dp", N, t_copy, "recv")
-    mean = jnp.sum(tbuf[...].astype(F32), axis=0) * (1.0 / N)
-    q_factor = jnp.dot(inverse, mean, precision=HI, preferred_element_type=F32).astype(BF16)
-
-    for c in range(width // chunk):
-        cols = pl.ds(c * chunk, chunk)
-        low = jnp.dot(bt_v[cols, :], q_factor, preferred_element_type=F32)
-        err_out[0, 0, cols, :] = (merged[cols, :] - low).astype(BF16)
-    wg_out[0] = jnp.dot(bt_v[pl.ds(pl.multiple_of(me * shard, 8), shard), :], q_factor,
-                        preferred_element_type=F32)
-
-    @pl.when(z > 0)
-    def _():
-        def piece(c):
-            back_wait(z, c)
-            add_back(z, z, c)
-        loop(C, piece, 0)
-
-    @pl.when(z < E - 1)
-    def _():
-        def piece(c):
-            back_wait(E, c)
-            add_back(z, E, c)
-        loop(C, piece, 0)
-    gt_out[...] = back[z]
-
+    relays(E - 1, E, 0, CB + lag)
     for d, dirn in enumerate((1, -1)):
         nb = z + dirn
         ahead = z if d == 0 else E - 1 - z
@@ -418,13 +374,38 @@
         loop(half, lambda k: w_copy(cross(k), me, k).wait_send())
         w_copy(partner, me, 0).wait_send()
         loop(half, lambda k: w_copy(partner, cross(k), half + k).wait_send())
+    each("dp", N, f_copy, "send")
+    each("dp", N, a_copy, "send")
+    each("dp", N, t_copy, "recv")
+    mean = jnp.sum(tbuf[...].astype(F32), axis=0) * (1.0 / N)
+    q_factor = jnp.dot(inverse, mean, precision=HI, preferred_element_type=F32).astype(BF16)
+
+    for c in range(width // chunk):
+        cols = pl.ds(c * chunk, chunk)
+        low = jnp.dot(bt_v[cols, :], q_factor, preferred_element_type=F32)
+        err_out[0, 0, cols, :] = (merged[cols, :] - low).astype(BF16)
+    wg_out[0] = jnp.dot(bt_v[pl.ds(pl.multiple_of(me * shard, 8), shard), :], q_factor,
+                        preferred_element_type=F32)
+
+    @pl.when(z > 0)
+    def _():
+        def piece(c):
+            back_wait(z, c)
+            add_back(z, z, c)
+        loop(CB, piece, 0)
+
+    @pl.when(z < E - 1)
+    def _():
+        def piece(c):
+            back_wait(E, c)
+            add_back(z, E, c)
+        loop(CB, piece, 0)
+    gt_out[...] = back[z]
 
     def sent(k):
         dest = other("expert", E, k)
-        loop(C, lambda c: back_copy(dest, c).wait_send(), 0)
+        loop(CB, lambda c: back_copy(dest, c).wait_send(), 0)
     loop(E, sent)
-    each("dp", N, f_copy, "send")
-    each("dp", N, a_copy, "send")
     each("dp", N, t_copy, "send")
 
 
@@ -438,7 +419,8 @@
     gather_w = shard % 16 == 0 and N & (N - 1) == 0
     weight = w_in[0] if gather_w else lax.all_gather(w_in[0], "dp", axis=0, tiled=True)
     chunk = 256 if width % 256 == 0 else 128
-    C = 4 if E <= 8 else 2
+    C, CB = (4, 8) if E <= 8 else (2, 2)
+    room = (4 * E + 3) * rows * width * 2 + 3 * E * rows * hidden * 2 + 13 * width * hidden + (12 << 20)
     total_rows = width // 128 * rank
     rp = -(-total_rows // N)
     rp = -(-rp // 8) * 8
@@ -446,7 +428,7 @@
     vmem = pl.BlockSpec(memory_space=pltpu.VMEM)
     hbm = pl.BlockSpec(memory_space=pltpu.HBM)
     return pl.pallas_call(
-        functools.partial(kernel, (E, N, rp, chunk, gather_w, C)),
+        functools.partial(kernel, (E, N, rp, chunk, gather_w, C, CB)),
         out_shape=(
             jax.ShapeDtypeStruct((rows, width), BF16),
             jax.ShapeDtypeStruct((1, 1, width, hidden), BF16),
@@ -481,11 +463,12 @@
             pltpu.VMEM((width, rank), BF16),
             dma((7,)), dma((2, E, C)), dma((E, C)), dma((E,)), dma((E,)), dma((E,)), dma((E,)),
             dma((N,)), dma((N,)), dma((N,)), dma((N,)), dma((N,)), dma((N,)), dma((N,)), dma((N,)),
-            dma((E, C)), dma((E + 1, C)),
+            dma((E, CB)), dma((E + 1, CB)),
         ],
         compiler_params=pltpu.CompilerParams(
-            collective_id=0, has_side_effects=True, vmem_limit_bytes=67043328 - (1 << 20)),
-    )(tokens, grad_hidden, routes.T, gates.T, weight, error, q_seed[0].T)
+            collective_id=0, has_side_effects=True, vmem_limit_bytes=min(room, 67043328 - (1 << 20))),
+    )(*(pltpu.with_memory_space_constraint(a, pltpu.HBM) for a in (
+        tokens, grad_hidden, routes.T, gates.T, weight, error, q_seed[0].T)))
 
 
 def solution(mesh):

time: 84.9 us -> 73.8 us (0.87)
  Pallas kernels: 78.5 us -> 70.2 us
  local copies, waits for them, and re-layouts: 5.49 us -> 2.76 us
    pallas_call x1, Pallas kernels: 78.5 us -> 70.2 us  [body(): pl.pallas_call(functools.partial(kernel, (E, N, rp, chunk, gather_w, C, C...]
    unnamed x5 -> x3, local copies, waits for them, and re-layouts: 5.49 us -> 2.76 us
where the time goes in v2:
time: 73.8 us; the launch traced here: 73.6 us
  Pallas kernels  70.2 us (95%)
  local copies, waits for them, and re-layouts  2.76 us (4%)
    pallas_call x1, Pallas kernels, body(): pl.pallas_call(functools.partial(kernel, (E, N, rp, chunk, gather_w, C, C...  70.2 us
    unnamed x3, local copies, waits for them, and re-layouts  2.76 us

profile of v2, /device:TPU:0, one launch (start us, length us, event | category | flops | bytes accessed | tf_op | source)
XLA Modules:
  0.0 73.6 jit_solution(12701939536716365000)
XLA Ops:
  0.6 70.2 %shard_map.94 = (bf16[128,1792]{1,0:T(8,128)(2,1)S(1)}, bf16[1,1,1792,512]{3,2,1,0:T(8,128)(2,1)S(1)}, f32[1,224,512]{2,1,0:T(8,128)S(1)}) custom-call(bf16[128,1792]{1,0:T(8,128)(2,1)} %tok_hbm.1, bf16[128,2,512]{2,1,0:T(2,128)(2,1)} %gh_hbm.1, s32[2,128]{1,0:T(2,128)} %bitcast.8, f32[2,128]{1,0:T(2,128)} %bitcast.9, bf16[224,512]{1,0:T(8,128)(2,1)} %bitcast.6, ...), custom_call_target="tpu_custom_call" | custom-call | tf_op jit(solution)/shard_map/pallas_call | solution.py:430
  70.9 0.8 %copy.13 = bf16[128,1792]{1,0:T(8,128)(2,1)} copy(bf16[128,1792]{1,0:T(8,128)(2,1)S(1)} %get-tuple-element.6) | data formatting | bytes 917504
  71.6 1.2 %copy.14 = bf16[1,1,1792,512]{3,2,1,0:T(8,128)(2,1)} copy(bf16[1,1,1792,512]{3,2,1,0:T(8,128)(2,1)S(1)} %get-tuple-element.7) | data formatting | bytes 3670016
  72.9 0.8 %copy.15 = f32[1,224,512]{2,1,0:T(8,128)} copy(f32[1,224,512]{2,1,0:T(8,128)S(1)} %get-tuple-element.8) | data formatting | bytes 917504

commit v3 on v2

--- a/solution.py
+++ b/solution.py
@@ -13,6 +13,38 @@
 BF16 = jnp.bfloat16
 NT = (((1,), (1,)), ((), ()))
 TN = (((0,), (0,)), ((), ()))
+
+
+PLAN = (
+    (
+        (("g", 1), ("g", 2), ("g", 3),),
+        (("w", 1, 0), ("w", 1, 1), ("w", 1, 2), ("w", 1, 3), ("W",), ("u", 1, 0, 1),),
+        (("u", 1, 1, 0),),
+        (("w", 2, 0), ("w", 2, 1), ("u", 0, 0, 1),),
+        (("u", 0, 1, 0),),
+        (("u", 2, 0, 1),),
+        (("w", 3, 0), ("w", 3, 1), ("u", 3, 0, 1),),
+        (("w", 3, 2), ("w", 3, 3), ("u", 3, 1, 0),),
+        (("w", 2, 2), ("w", 2, 3), ("u", 2, 1, 0),),
+    ),
+    (
+        (("g", 0), ("g", 2), ("g", 3),),
+        (("w", 0, 0), ("r", 1, 0, 0), ("w", 2, 0), ("r", -1, 2, 0), ("w", 0, 1), ("r", 1, 0, 1), ("w", 2, 1), ("r", -1, 2, 1), ("w", 0, 2), ("r", 1, 0, 2), ("w", 2, 2), ("w", 0, 3), ("r", 1, 0, 3), ("w", 2, 3), ("W",), ("u", 1, 0, 1),),
+        (("u", 1, 1, 0),),
+        (("u", 0, 0, 1),),
+        (("u", 0, 1, 0),),
+        (("u", 2, 0, 1),),
+        (("u", 2, 1, 0),),
+        (("w", 3, 0), ("r", -1, 3, 0), ("w", 3, 1), ("r", -1, 3, 1), ("u", 3, 0, 1),),
+        (("w", 3, 2), ("r", -1, 3, 2), ("w", 3, 3), ("r", -1, 3, 3), ("r", -1, 2, 2), ("r", -1, 2, 3), ("u", 3, 1, 0),),
+    ),
+)
+RELAYS = (
+    (2, 0), (2, 1), (2, 2), (2, 3), (3, 0), (3, 1), (3, 2), (3, 3),
+    (0, 0), (3, 4), (0, 1), (3, 5), (0, 2), (3, 6), (0, 3), (3, 7),
+    (0, 4), (0, 5), (0, 6), (0, 7), (2, 4), (2, 5), (2, 6), (2, 7),
+)
+STOPS = (4, 6, 8)
 
 
 def slopes(pre_act):
@@ -111,7 +143,7 @@
 
     def tok_copy(j, c, nb, d):
         piece = tok_all.at[j, rows_of(c)]
-        return rdma(piece, piece, tok_s.at[d, j, c], tok_r.at[j, c], "expert", nb)
+        return rdma(piece, piece, tok_s.at[d, j], tok_r.at[j, c], "expert", nb)
 
     def w_copy(p, slot, k):
         return rdma(w_rows(slot), w_rows(slot), w_s.at[k], w_r.at[slot], "dp", p)
@@ -171,13 +203,43 @@
         choose = jnp.where(wanted == e.astype(F32), 1.0, 0.0).astype(BF16)
         gh_sel[e] = jnp.dot(choose, pairs, preferred_element_type=F32).astype(BF16)
 
-    def send_rows(k):
-        p = other("expert", E, k)
-        pick_rows(p)
-        gh_copy(p, z, k).start()
-    loop(E, send_rows)
-    pick_rows(z)
+    def gh_send(p):
+        gh_copy(p, z, lax.rem(p - z + E, E)).start()
+
+    loop(E, pick_rows, 0)
     gh_all[z] = gh_sel[z]
+
+    def mirrored(value):
+        return jnp.where(z < E - 1 - z, value, E - 1 - value)
+
+    def act(op):
+        kind = op[0]
+        if kind == "g":
+            gh_send(mirrored(op[1]))
+        elif kind == "w":
+            tok_copy(mirrored(op[1]), op[2], z, 0).wait_recv()
+        elif kind == "r":
+            dirn = jnp.where(z < E - 1 - z, op[1], -op[1])
+            tok_copy(mirrored(op[2]), op[3], z + dirn, jnp.where(dirn > 0, 0, 1)).start()
+        elif gather_w:
+            weights()
+
+    def acts(pick):
+        for low in range(E // 2):
+            @pl.when((z == low) | (z == E - 1 - low))
+            def _():
+                pick(low)
+
+    def look(table, k):
+        code = table[0]
+        for n in range(1, len(table)):
+            code = jnp.where(k == n, table[n], code)
+        return code
+
+    if E == len(PLAN) * 2:
+        acts(lambda low: [act(op) for op in PLAN[low][0]])
+    else:
+        loop(E, lambda k: gh_send(other("expert", E, k)))
 
     loads[5].wait()
     loads[6].wait()
@@ -197,10 +259,10 @@
         nb = z + dirn
         slot = jnp.where((dest == nb) & (dest < z), E, dest)
         return rdma(back.at[dest, back_rows(c)], ret.at[slot, back_rows(c)],
-                    b_s.at[dest, c], b_r.at[slot, c], "expert", nb)
+                    b_s.at[dest], b_r.at[slot, c], "expert", nb)
 
     def back_wait(slot, c):
-        rdma(back.at[0, back_rows(c)], ret.at[slot, back_rows(c)], b_s.at[0, c], b_r.at[slot, c],
+        rdma(back.at[0, back_rows(c)], ret.at[slot, back_rows(c)], b_s.at[0], b_r.at[slot, c],
              "expert", other("expert", E, 1)).wait_recv()
 
     def add_back(dest, slot, c):
@@ -208,29 +270,38 @@
         back[dest, rows, :] = (back[dest, rows, :].astype(F32)
                                + ret[slot, rows, :].astype(F32)).astype(BF16)
 
-    def gate_column(j):
-        return jnp.transpose(gate_all[j])[:, :1]
-
-    def inward(j):
-        @pl.when(j != z)
+    unit = tokens // 2
+
+    def unit_rows(h):
+        return pl.ds(pl.multiple_of(h * unit, 16), unit)
+
+    def gate_column(j, h):
+        column = jnp.transpose(gate_all[j])[:, :1]
+        return jnp.where(h == 0, column[:unit], column[unit:])
+
+    def inward(j, h, fresh):
+        @pl.when((j != z) & fresh)
         def _():
             gate_copy(j, j, 0).wait_recv()
             gh_copy(j, j, 0).wait_recv()
-        x = (tok_all[j].astype(F32) * gate_column(j)).astype(BF16)
-        x_all[j] = x
+        rows = unit_rows(h)
+        x = (tok_all[j, rows, :].astype(F32) * gate_column(j, h)).astype(BF16)
+        x_all[j, rows, :] = x
         pre = jnp.dot(x, w_all[...], preferred_element_type=F32)
-        gp = (gh_all[j].astype(F32) * slopes(pre)).astype(BF16)
-        gp_all[j] = gp
+        gp = (gh_all[j, rows, :].astype(F32) * slopes(pre)).astype(BF16)
+        gp_all[j, rows, :] = gp
         seen = fold(lax.dot_general(q2[...], gp, NT, preferred_element_type=F32))
         facc[...] += fold(jnp.dot(halves(seen), x, preferred_element_type=F32))
 
-    def outward(j):
-        back[j] = (lax.dot_general(gp_all[j], w_all[...], NT, preferred_element_type=F32)
-                   * gate_column(j)).astype(BF16)
+    def outward(j, h):
+        rows = unit_rows(h)
+        back[j, rows, :] = (lax.dot_general(gp_all[j, rows, :], w_all[...], NT,
+                                            preferred_element_type=F32)
+                            * gate_column(j, h)).astype(BF16)
 
         @pl.when(((j > z) & (z == 0)) | ((j < z) & (z == E - 1)))
         def _():
-            loop(CB, lambda c: back_copy(j, c).start(), 0)
+            loop(CB // 2, lambda c: back_copy(j, h * (CB // 2) + c).start(), 0)
 
     def forward(s):
         def piece(c):
@@ -255,57 +326,76 @@
         w_copy(partner, partner, 0).wait_recv()
         loop(half, lambda k: w_copy(partner, partner + cross(k) - me, 0).wait_recv())
 
-    farthest = jnp.maximum(z, E - 1 - z)
-
-    def step(s):
-        forward(s)
-        if gather_w:
-            @pl.when(s == 1)
+    if E == len(PLAN) * 2:
+        turns = len(PLAN[0]) - 1
+
+        def unit_at(k):
+            codes = [[4 * op[1] + 2 * op[2] + op[3] for op in (turn[-1] for turn in side[1:])]
+                     for side in PLAN]
+            code = jnp.where((z == 0) | (z == E - 1), look(codes[0], k), look(codes[1], k))
+            return mirrored(code // 4), lax.rem(code // 2, 2), lax.rem(code, 2) == 1
+
+        def turn(k):
+            def moves(low):
+                for n in range(turns):
+                    ops = PLAN[low][n + 1][:-1]
+                    if ops:
+                        @pl.when(k == n)
+                        def _():
+                            for op in ops:
+                                act(op)
+            acts(moves)
+            j, h, fresh = unit_at(k)
+            inward(j, h, fresh)
+
+            @pl.when(k < turns - 1)
             def _():
-                weights()
-
-        def block(i, carry):
-            j = jnp.where(i == 0, z, jnp.where(i == 1, z - s, z + s))
-
-            @pl.when((j >= 0) & (j < E) & ((i > 0) | (s == 1)))
-            def _():
-                inward(j)
-
-                @pl.when((s < farthest) | (i == 0))
+                outward(j, h)
+        loop(turns, turn, 0)
+    else:
+        def step(s):
+            forward(s)
+            if gather_w:
+                @pl.when(s == 1)
                 def _():
-                    outward(j)
-            return carry
-        lax.fori_loop(0, 3, block, 0)
-    loop(E, step)
+                    weights()
+
+            def block(i, carry):
+                side = i // 2
+                h = lax.rem(i, 2)
+                j = jnp.where(side == 0, z, jnp.where(side == 1, z - s, z + s))
+
+                @pl.when((j >= 0) & (j < E) & ((side > 0) | (s == 1)))
+                def _():
+                    inward(j, h, h == 0)
+                    outward(j, h)
+                return carry
+            lax.fori_loop(0, 6, block, 0)
+        loop(E, step)
 
     if fbuf.shape[0] > groups * rank:
-        fbuf[...] = jnp.zeros_like(fbuf)
+        fbuf[groups * rank :, :] = jnp.zeros((fbuf.shape[0] - groups * rank, 128), BF16)
     for c in range(groups):
-        fbuf[c * rank : (c + 1) * rank, :] = facc[:, c * 128 : (c + 1) * 128]
+        fbuf[c * rank : (c + 1) * rank, :] = facc[:, c * 128 : (c + 1) * 128].astype(BF16)
 
     def f_copy(p, slot, k):
-        return rdma(fbuf.at[pl.ds(pl.multiple_of(p * rp, 8), rp)], rsbuf.at[slot],
+        return rdma(fbuf.at[pl.ds(pl.multiple_of(p * rp, 16), rp)], rsbuf.at[slot],
                     f_s.at[k], f_r.at[slot], "dp", p)
 
     def a_copy(p, slot, k):
-        piece = agbuf.at[pl.ds(pl.multiple_of(slot * rp, 8), rp)]
+        piece = agbuf.at[pl.ds(pl.multiple_of(slot * rp, 16), rp)]
         return rdma(piece, piece, a_s.at[k], a_r.at[slot], "dp", p)
 
     def t_copy(p, slot, k):
         return rdma(tbuf.at[slot], tbuf.at[slot], t_s.at[k], t_r.at[slot], "dp", p)
 
-    own = pl.ds(pl.multiple_of(me * rp, 8), rp)
+    own = pl.ds(pl.multiple_of(me * rp, 16), rp)
     each("dp", N, f_copy, "start")
     rsbuf[me] = fbuf[own, :]
 
-    def last_block(i, carry):
-        j = jnp.where(i == 0, z - farthest, z + farthest)
-
-        @pl.when((j >= 0) & (j < E))
-        def _():
-            outward(j)
-        return carry
-    lax.fori_loop(0, 2, last_block, 0)
+    if E == len(PLAN) * 2:
+        j, h, _ = unit_at(turns - 1)
+        outward(j, h)
 
     right_first = z < E - 1 - z
     lag = 3
@@ -324,6 +414,19 @@
                 back_copy(dest, piece).start()
             return carry
         lax.fori_loop(0, 2, turn, 0)
+
+    def planned(start, stop):
+        @pl.when((z > 0) & (z < E - 1))
+        def _():
+            def one(i, carry):
+                code = look([CB * op[0] + op[1] for op in RELAYS], i)
+                dest = mirrored(code // CB)
+                piece = lax.rem(code, CB)
+                back_wait(dest, piece)
+                add_back(dest, dest, piece)
+                back_copy(dest, piece).start()
+                return carry
+            lax.fori_loop(start, stop, one, 0)
 
     def relays(start, stop, first, last):
         def rank_of(m, carry):
@@ -339,24 +442,35 @@
         m = m + err_v[cols, :].astype(F32)
         merged[cols, :] = m
         merged_b[cols, :] = m.astype(BF16)
+    if E == len(PLAN) * 2:
+        planned(0, STOPS[0])
+    else:
+        relays(1, E - 1, 0, CB // 2)
+    each("dp", N, f_copy, "recv")
+    agbuf[own, :] = (jnp.sum(rsbuf[...].astype(F32), axis=0) * (1.0 / N)).astype(BF16)
+    each("dp", N, a_copy, "start")
     loop(width // chunk, merge, 0)
-    relays(1, E - 1, 0, CB // 2)
-    each("dp", N, f_copy, "recv")
-    agbuf[own, :] = jnp.sum(rsbuf[...], axis=0) * (1.0 / N)
-    each("dp", N, a_copy, "start")
-
-    relays(1, E - 1, CB // 2, CB + lag)
+
+    if E == len(PLAN) * 2:
+        planned(STOPS[0], STOPS[1])
+    else:
+        relays(1, E - 1, CB // 2, CB + lag)
     each("dp", N, a_copy, "recv")
     factor = jnp.concatenate([agbuf[c * rank : (c + 1) * rank, :] for c in range(groups)], axis=1)
-    tbuf[me] = fold(jnp.dot(halves(factor), merged_b[...], preferred_element_type=F32)).astype(BF16)
+    tbuf[me] = jnp.dot(factor, merged_b[...], preferred_element_type=F32).astype(BF16)
     each("dp", N, t_copy, "start")
 
-    gram = lax.dot_general(factor, factor, NT, precision=HI, preferred_element_type=F32)
+    if E == len(PLAN) * 2:
+        planned(STOPS[1], STOPS[2])
+    gram = lax.dot_general(factor, factor, NT, preferred_element_type=F32)
     inverse = inverse_factor(gram)
-    basis = jnp.dot(inverse, factor, precision=HI, preferred_element_type=F32)
+    basis = fold(jnp.dot(halves(inverse), factor, preferred_element_type=F32))
     bt_v[...] = jnp.transpose(basis).astype(BF16)
 
-    relays(E - 1, E, 0, CB + lag)
+    if E == len(PLAN) * 2:
+        planned(STOPS[2], len(RELAYS))
+    else:
+        relays(E - 1, E, 0, CB + lag)
     for d, dirn in enumerate((1, -1)):
         nb = z + dirn
         ahead = z if d == 0 else E - 1 - z
@@ -366,7 +480,9 @@
             def drain(s):
                 @pl.when(s <= ahead)
                 def _():
-                    loop(C, lambda c: tok_copy(z - dirn * s, c, nb, d).wait_send(), 0)
+                    j = z - dirn * s
+                    rdma(tok_all.at[j], tok_all.at[j], tok_s.at[d, j], tok_r.at[j, 0],
+                         "expert", nb).wait_send()
             loop(E, drain, 0)
     each("expert", E, gate_copy, "send")
     each("expert", E, gh_copy, "send")
@@ -404,7 +520,8 @@
 
     def sent(k):
         dest = other("expert", E, k)
-        loop(CB, lambda c: back_copy(dest, c).wait_send(), 0)
+        rdma(back.at[dest], ret.at[dest], b_s.at[dest], b_r.at[dest, 0], "expert",
+             other("expert", E, 1)).wait_send()
     loop(E, sent)
     each("dp", N, t_copy, "send")
 
@@ -423,7 +540,7 @@
     room = (4 * E + 3) * rows * width * 2 + 3 * E * rows * hidden * 2 + 13 * width * hidden + (12 << 20)
     total_rows = width // 128 * rank
     rp = -(-total_rows // N)
-    rp = -(-rp // 8) * 8
+    rp = -(-rp // 16) * 16
     dma = pltpu.SemaphoreType.DMA
     vmem = pl.BlockSpec(memory_space=pltpu.VMEM)
     hbm = pl.BlockSpec(memory_space=pltpu.HBM)
@@ -456,14 +573,14 @@
             pltpu.VMEM((rank, hidden), F32),
             pltpu.VMEM((2 * rank, hidden), BF16),
             pltpu.VMEM((rank, width), F32),
-            pltpu.VMEM((rp * N, 128), F32),
-            pltpu.VMEM((N, rp, 128), F32),
-            pltpu.VMEM((rp * N, 128), F32),
+            pltpu.VMEM((rp * N, 128), BF16),
+            pltpu.VMEM((N, rp, 128), BF16),
+            pltpu.VMEM((rp * N, 128), BF16),
             pltpu.VMEM((N, rank, hidden), BF16),
             pltpu.VMEM((width, rank), BF16),
-            dma((7,)), dma((2, E, C)), dma((E, C)), dma((E,)), dma((E,)), dma((E,)), dma((E,)),
+            dma((7,)), dma((2, E)), dma((E, C)), dma((E,)), dma((E,)), dma((E,)), dma((E,)),
             dma((N,)), dma((N,)), dma((N,)), dma((N,)), dma((N,)), dma((N,)), dma((N,)), dma((N,)),
-            dma((E, CB)), dma((E + 1, CB)),
+            dma((E,)), dma((E + 1, CB)),
         ],
         compiler_params=pltpu.CompilerParams(
             collective_id=0, has_side_effects=True, vmem_limit_bytes=min(room, 67043328 - (1 << 20))),

time: 73.8 us -> 66.9 us (0.907)
  Pallas kernels: 70.2 us -> 63.3 us
    pallas_call x1, Pallas kernels: 70.2 us -> 63.3 us  [body(): pl.pallas_call(functools.partial(kernel, (E, N, rp, chunk, gather_w, C, C...]
where the time goes in v3:
time: 66.9 us; the launch traced here: 66.7 us
  Pallas kernels  63.3 us (95%)
  local copies, waits for them, and re-layouts  2.76 us (4%)
    pallas_call x1, Pallas kernels, body(): pl.pallas_call(functools.partial(kernel, (E, N, rp, chunk, gather_w, C, C...  63.3 us
    unnamed x3, local copies, waits for them, and re-layouts  2.76 us

profile of v3, /device:TPU:0, one launch (start us, length us, event | category | flops | bytes accessed | tf_op | source)
XLA Modules:
  0.0 66.7 jit_solution(8187347484888617292)
XLA Ops:
  0.6 63.3 %shard_map.94 = (bf16[128,1792]{1,0:T(8,128)(2,1)S(1)}, bf16[1,1,1792,512]{3,2,1,0:T(8,128)(2,1)S(1)}, f32[1,224,512]{2,1,0:T(8,128)S(1)}) custom-call(bf16[128,1792]{1,0:T(8,128)(2,1)} %tok_hbm.1, bf16[128,2,512]{2,1,0:T(2,128)(2,1)} %gh_hbm.1, s32[2,128]{1,0:T(2,128)} %bitcast.8, f32[2,128]{1,0:T(2,128)} %bitcast.9, bf16[224,512]{1,0:T(8,128)(2,1)} %bitcast.6, ...), custom_call_target="tpu_custom_call" | custom-call | tf_op jit(solution)/shard_map/pallas_call | solution.py:547
  63.9 0.8 %copy.13 = bf16[128,1792]{1,0:T(8,128)(2,1)} copy(bf16[128,1792]{1,0:T(8,128)(2,1)S(1)} %get-tuple-element.6) | data formatting | bytes 917504
  64.7 1.2 %copy.14 = bf16[1,1,1792,512]{3,2,1,0:T(8,128)(2,1)} copy(bf16[1,1,1792,512]{3,2,1,0:T(8,128)(2,1)S(1)} %get-tuple-element.7) | data formatting | bytes 3670016
  65.9 0.8 %copy.15 = f32[1,224,512]{2,1,0:T(8,128)} copy(f32[1,224,512]{2,1,0:T(8,128)S(1)} %get-tuple-element.8) | data formatting | bytes 917504

commit v4 on v3

--- a/solution.py
+++ b/solution.py
@@ -20,31 +20,31 @@
         (("g", 1), ("g", 2), ("g", 3),),
         (("w", 1, 0), ("w", 1, 1), ("w", 1, 2), ("w", 1, 3), ("W",), ("u", 1, 0, 1),),
         (("u", 1, 1, 0),),
-        (("w", 2, 0), ("w", 2, 1), ("u", 0, 0, 1),),
+        (("u", 0, 0, 1),),
         (("u", 0, 1, 0),),
-        (("u", 2, 0, 1),),
+        (("w", 2, 0), ("w", 2, 1), ("u", 2, 0, 1),),
         (("w", 3, 0), ("w", 3, 1), ("u", 3, 0, 1),),
         (("w", 3, 2), ("w", 3, 3), ("u", 3, 1, 0),),
         (("w", 2, 2), ("w", 2, 3), ("u", 2, 1, 0),),
     ),
     (
         (("g", 0), ("g", 2), ("g", 3),),
-        (("w", 0, 0), ("r", 1, 0, 0), ("w", 2, 0), ("r", -1, 2, 0), ("w", 0, 1), ("r", 1, 0, 1), ("w", 2, 1), ("r", -1, 2, 1), ("w", 0, 2), ("r", 1, 0, 2), ("w", 2, 2), ("w", 0, 3), ("r", 1, 0, 3), ("w", 2, 3), ("W",), ("u", 1, 0, 1),),
+        (("w", 0, 0), ("r", 1, 0, 0), ("w", 2, 0), ("r", -1, 2, 0), ("w", 0, 1), ("r", 1, 0, 1), ("w", 2, 1), ("r", -1, 2, 1), ("w", 0, 2), ("r", 1, 0, 2), ("w", 2, 2), ("r", -1, 2, 2), ("w", 0, 3), ("r", 1, 0, 3), ("w", 2, 3), ("W",), ("u", 1, 0, 1),),
         (("u", 1, 1, 0),),
         (("u", 0, 0, 1),),
         (("u", 0, 1, 0),),
         (("u", 2, 0, 1),),
         (("u", 2, 1, 0),),
         (("w", 3, 0), ("r", -1, 3, 0), ("w", 3, 1), ("r", -1, 3, 1), ("u", 3, 0, 1),),
-        (("w", 3, 2), ("r", -1, 3, 2), ("w", 3, 3), ("r", -1, 3, 3), ("r", -1, 2, 2), ("r", -1, 2, 3), ("u", 3, 1, 0),),
+        (("w", 3, 2), ("r", -1, 3, 2), ("w", 3, 3), ("r", -1, 3, 3), ("r", -1, 2, 3), ("u", 3, 1, 0),),
     ),
 )
 RELAYS = (
     (2, 0), (2, 1), (2, 2), (2, 3), (3, 0), (3, 1), (3, 2), (3, 3),
     (0, 0), (3, 4), (0, 1), (3, 5), (0, 2), (3, 6), (0, 3), (3, 7),
-    (0, 4), (0, 5), (0, 6), (0, 7), (2, 4), (2, 5), (2, 6), (2, 7),
+    (0, 4), (2, 4), (0, 5), (2, 5), (0, 6), (2, 6), (0, 7), (2, 7),
 )
-STOPS = (4, 6, 8)
+STOPS = (4, 7, 9, 11, 13, 15)
 
 
 def slopes(pre_act):
@@ -63,7 +63,7 @@
     return value[:rows] + value[rows:]
 
 
-def inverse_factor(gram):
+def inverse_factor(gram, between):
     rank = gram.shape[0]
     rows = lax.broadcasted_iota(jnp.int32, (rank, rank), 0)
     cols = lax.broadcasted_iota(jnp.int32, (rank, rank), 1)
@@ -77,14 +77,16 @@
         row_r = right[i : i + 1, :] * scale
         left = left - col * row_l
         right = right - col * row_r
+        if i % 8 == 7:
+            between(i // 8)
     pivots = jnp.sum(jnp.where(rows == cols, left, 0.0), axis=1, keepdims=True)
     return right * (1.0 / jnp.sqrt(pivots))
 
 
 def kernel(dims, tok_hbm, gh_hbm, rt_hbm, gt_hbm, w_hbm, err_hbm, q_hbm,
-           gt_out, err_out, wg_out,
+           gt_out, merged, bt_v, q_out,
            tok_all, gh_raw, gh_sel, gh_all, rt_v, gt_v, gate_sel, gate_all, w_all, x_all, gp_all,
-           err_v, merged, merged_b, back, ret, q_v, q2, facc, fbuf, rsbuf, agbuf, tbuf, bt_v,
+           err_v, merged_b, back, ret, q_v, q2, facc, fbuf, rsbuf, agbuf, tbuf,
            in_s, tok_s, tok_r, gh_s, gh_r, gate_s, gate_r, w_s, w_r,
            f_s, f_r, a_s, a_r, t_s, t_r, b_s, b_r):
     E, N, rp, chunk, gather_w, C, CB = dims
@@ -107,10 +109,10 @@
         lax.fori_loop(start, size, step, 0)
 
     barrier = pltpu.get_barrier_semaphore()
-    loop(E, lambda k: pl.semaphore_signal(
-        barrier, inc=1, device_id={"expert": other("expert", E, k)}, device_id_type=MESH))
-    loop(N, lambda k: pl.semaphore_signal(
-        barrier, inc=1, device_id={"dp": other("dp", N, k)}, device_id_type=MESH))
+    for axis, size in (("expert", E), ("dp", N)):
+        for k in range(1, size):
+            pl.semaphore_signal(barrier, inc=1, device_id={axis: other(axis, size, k)},
+                                device_id_type=MESH)
 
     def w_rows(slot):
         return w_all.at[pl.ds(pl.multiple_of(slot * shard, 16), shard)] if gather_w else w_all
@@ -133,10 +135,10 @@
             device_id={axis: peer}, device_id_type=MESH)
 
     def gate_copy(p, slot, k):
-        return rdma(gate_sel.at[p], gate_all.at[slot], gate_s.at[k], gate_r.at[slot], "expert", p)
+        return rdma(gate_sel.at[p], gate_all.at[slot], gate_s, gate_r.at[slot], "expert", p)
 
     def gh_copy(p, slot, k):
-        return rdma(gh_sel.at[p], gh_all.at[slot], gh_s.at[k], gh_r.at[slot], "expert", p)
+        return rdma(gh_sel.at[p], gh_all.at[slot], gh_s, gh_r.at[slot], "expert", p)
 
     def rows_of(c):
         return pl.ds(pl.multiple_of(c * part, 16), part)
@@ -146,7 +148,7 @@
         return rdma(piece, piece, tok_s.at[d, j], tok_r.at[j, c], "expert", nb)
 
     def w_copy(p, slot, k):
-        return rdma(w_rows(slot), w_rows(slot), w_s.at[k], w_r.at[slot], "dp", p)
+        return rdma(w_rows(slot), w_rows(slot), w_s, w_r.at[slot], "dp", p)
 
     def each(p_axis, size, copy, act):
         mine = lax.axis_index(p_axis)
@@ -221,6 +223,8 @@
         elif kind == "r":
             dirn = jnp.where(z < E - 1 - z, op[1], -op[1])
             tok_copy(mirrored(op[2]), op[3], z + dirn, jnp.where(dirn > 0, 0, 1)).start()
+        elif kind == "x":
+            pass_on(mirrored(op[1]), op[2])
         elif gather_w:
             weights()
 
@@ -269,6 +273,11 @@
         rows = back_rows(c)
         back[dest, rows, :] = (back[dest, rows, :].astype(F32)
                                + ret[slot, rows, :].astype(F32)).astype(BF16)
+
+    def pass_on(dest, piece):
+        back_wait(dest, piece)
+        add_back(dest, dest, piece)
+        back_copy(dest, piece).start()
 
     unit = tokens // 2
 
@@ -380,14 +389,24 @@
 
     def f_copy(p, slot, k):
         return rdma(fbuf.at[pl.ds(pl.multiple_of(p * rp, 16), rp)], rsbuf.at[slot],
-                    f_s.at[k], f_r.at[slot], "dp", p)
+                    f_s, f_r, "dp", p)
 
     def a_copy(p, slot, k):
         piece = agbuf.at[pl.ds(pl.multiple_of(slot * rp, 16), rp)]
-        return rdma(piece, piece, a_s.at[k], a_r.at[slot], "dp", p)
+        return rdma(piece, piece, a_s, a_r, "dp", p)
 
     def t_copy(p, slot, k):
-        return rdma(tbuf.at[slot], tbuf.at[slot], t_s.at[k], t_r.at[slot], "dp", p)
+        return rdma(tbuf.at[slot], tbuf.at[slot], t_s, t_r, "dp", p)
+
+    def all_f():
+        return rdma(rsbuf.at[pl.ds(0, N - 1)], rsbuf.at[pl.ds(0, N - 1)], f_s, f_r, "dp", partner)
+
+    def all_a():
+        rest = agbuf.at[pl.ds(0, rp * (N - 1))]
+        return rdma(rest, rest, a_s, a_r, "dp", partner)
+
+    def all_t():
+        return rdma(tbuf.at[pl.ds(0, N - 1)], tbuf.at[pl.ds(0, N - 1)], t_s, t_r, "dp", partner)
 
     own = pl.ds(pl.multiple_of(me * rp, 16), rp)
     each("dp", N, f_copy, "start")
@@ -420,11 +439,7 @@
         def _():
             def one(i, carry):
                 code = look([CB * op[0] + op[1] for op in RELAYS], i)
-                dest = mirrored(code // CB)
-                piece = lax.rem(code, CB)
-                back_wait(dest, piece)
-                add_back(dest, dest, piece)
-                back_copy(dest, piece).start()
+                pass_on(mirrored(code // CB), lax.rem(code, CB))
                 return carry
             lax.fori_loop(start, stop, one, 0)
 
@@ -446,7 +461,7 @@
         planned(0, STOPS[0])
     else:
         relays(1, E - 1, 0, CB // 2)
-    each("dp", N, f_copy, "recv")
+    all_f().wait_recv()
     agbuf[own, :] = (jnp.sum(rsbuf[...].astype(F32), axis=0) * (1.0 / N)).astype(BF16)
     each("dp", N, a_copy, "start")
     loop(width // chunk, merge, 0)
@@ -455,7 +470,7 @@
         planned(STOPS[0], STOPS[1])
     else:
         relays(1, E - 1, CB // 2, CB + lag)
-    each("dp", N, a_copy, "recv")
+    all_a().wait_recv()
     factor = jnp.concatenate([agbuf[c * rank : (c + 1) * rank, :] for c in range(groups)], axis=1)
     tbuf[me] = jnp.dot(factor, merged_b[...], preferred_element_type=F32).astype(BF16)
     each("dp", N, t_copy, "start")
@@ -463,12 +478,15 @@
     if E == len(PLAN) * 2:
         planned(STOPS[1], STOPS[2])
     gram = lax.dot_general(factor, factor, NT, preferred_element_type=F32)
-    inverse = inverse_factor(gram)
+    def between(n):
+        if E == len(PLAN) * 2 and n + 3 < len(STOPS):
+            planned(STOPS[n + 2], STOPS[n + 3])
+    inverse = inverse_factor(gram, between)
     basis = fold(jnp.dot(halves(inverse), factor, preferred_element_type=F32))
     bt_v[...] = jnp.transpose(basis).astype(BF16)
 
     if E == len(PLAN) * 2:
-        planned(STOPS[2], len(RELAYS))
+        planned(STOPS[-1], len(RELAYS))
     else:
         relays(E - 1, E, 0, CB + lag)
     for d, dirn in enumerate((1, -1)):
@@ -484,24 +502,18 @@
                     rdma(tok_all.at[j], tok_all.at[j], tok_s.at[d, j], tok_r.at[j, 0],
                          "expert", nb).wait_send()
             loop(E, drain, 0)
-    each("expert", E, gate_copy, "send")
-    each("expert", E, gh_copy, "send")
+    rdma(gate_sel.at[pl.ds(0, E - 1)], gate_all.at[pl.ds(0, E - 1)], gate_s, gate_r.at[0],
+         "expert", other("expert", E, 1)).wait_send()
+    rdma(gh_sel.at[pl.ds(0, E - 1)], gh_all.at[pl.ds(0, E - 1)], gh_s, gh_r.at[0],
+         "expert", other("expert", E, 1)).wait_send()
     if gather_w:
-        loop(half, lambda k: w_copy(cross(k), me, k).wait_send())
-        w_copy(partner, me, 0).wait_send()
-        loop(half, lambda k: w_copy(partner, cross(k), half + k).wait_send())
-    each("dp", N, f_copy, "send")
-    each("dp", N, a_copy, "send")
-    each("dp", N, t_copy, "recv")
+        rest = w_all.at[pl.ds(0, shard * (N - 1))]
+        rdma(rest, rest, w_s, w_r.at[0], "dp", partner).wait_send()
+    all_f().wait_send()
+    all_a().wait_send()
+    all_t().wait_recv()
     mean = jnp.sum(tbuf[...].astype(F32), axis=0) * (1.0 / N)
-    q_factor = jnp.dot(inverse, mean, precision=HI, preferred_element_type=F32).astype(BF16)
-
-    for c in range(width // chunk):
-        cols = pl.ds(c * chunk, chunk)
-        low = jnp.dot(bt_v[cols, :], q_factor, preferred_element_type=F32)
-        err_out[0, 0, cols, :] = (merged[cols, :] - low).astype(BF16)
-    wg_out[0] = jnp.dot(bt_v[pl.ds(pl.multiple_of(me * shard, 8), shard), :], q_factor,
-                        preferred_element_type=F32)
+    q_out[...] = jnp.dot(inverse, mean, precision=HI, preferred_element_type=F32).astype(BF16)
 
     @pl.when(z > 0)
     def _():
@@ -523,7 +535,28 @@
         rdma(back.at[dest], ret.at[dest], b_s.at[dest], b_r.at[dest, 0], "expert",
              other("expert", E, 1)).wait_send()
     loop(E, sent)
-    each("dp", N, t_copy, "send")
+    all_t().wait_send()
+
+
+def finish(chunk, gt_v, merged, bt_v, q_v, gt_hbm, err_hbm, wg_hbm, err_v, wg_v, sem):
+    width = merged.shape[0]
+    shard = wg_v.shape[0]
+    me = lax.axis_index("dp")
+    count = width // chunk
+    moves = [pltpu.make_async_copy(gt_v, gt_hbm, sem.at[0])]
+    moves[0].start()
+    wg_v[...] = jnp.dot(bt_v[pl.ds(pl.multiple_of(me * shard, 8), shard), :], q_v[...],
+                        preferred_element_type=F32)
+    moves.append(pltpu.make_async_copy(wg_v, wg_hbm.at[0], sem.at[1]))
+    moves[1].start()
+    for c in range(count):
+        rows = pl.ds(c * chunk, chunk)
+        low = jnp.dot(bt_v[rows, :], q_v[...], preferred_element_type=F32)
+        err_v[rows, :] = (merged[rows, :] - low).astype(BF16)
+        moves.append(pltpu.make_async_copy(err_v.at[rows], err_hbm.at[0, 0, rows], sem.at[2 + c]))
+        moves[-1].start()
+    for move in moves:
+        move.wait()
 
 
 def body(tokens, routes, gates, grad_hidden, w_in, error, q_seed):
@@ -544,15 +577,16 @@
     dma = pltpu.SemaphoreType.DMA
     vmem = pl.BlockSpec(memory_space=pltpu.VMEM)
     hbm = pl.BlockSpec(memory_space=pltpu.HBM)
-    return pl.pallas_call(
+    parts = pl.pallas_call(
         functools.partial(kernel, (E, N, rp, chunk, gather_w, C, CB)),
         out_shape=(
             jax.ShapeDtypeStruct((rows, width), BF16),
-            jax.ShapeDtypeStruct((1, 1, width, hidden), BF16),
-            jax.ShapeDtypeStruct((1, shard, hidden), F32),
+            jax.ShapeDtypeStruct((width, hidden), F32),
+            jax.ShapeDtypeStruct((width, rank), BF16),
+            jax.ShapeDtypeStruct((rank, hidden), BF16),
         ),
         in_specs=[hbm] * 7,
-        out_specs=(vmem, vmem, vmem),
+        out_specs=(vmem,) * 4,
         scratch_shapes=[
             pltpu.VMEM((E, rows, width), BF16),
             pltpu.VMEM((rows, 2, hidden), BF16),
@@ -566,7 +600,6 @@
             pltpu.VMEM((E, rows, width), BF16),
             pltpu.VMEM((E, rows, hidden), BF16),
             pltpu.VMEM((width, hidden), BF16),
-            pltpu.VMEM((width, hidden), F32),
             pltpu.VMEM((width, hidden), BF16),
             pltpu.VMEM((E, rows, width), BF16),
             pltpu.VMEM((E + 1, rows, width), BF16),
@@ -577,15 +610,30 @@
             pltpu.VMEM((N, rp, 128), BF16),
             pltpu.VMEM((rp * N, 128), BF16),
             pltpu.VMEM((N, rank, hidden), BF16),
-            pltpu.VMEM((width, rank), BF16),
-            dma((7,)), dma((2, E)), dma((E, C)), dma((E,)), dma((E,)), dma((E,)), dma((E,)),
-            dma((N,)), dma((N,)), dma((N,)), dma((N,)), dma((N,)), dma((N,)), dma((N,)), dma((N,)),
+            dma((7,)), dma((2, E)), dma((E, C)), dma(()), dma((E,)), dma(()), dma((E,)),
+            dma(()), dma((N,)), dma(()), dma(()), dma(()), dma(()), dma(()), dma(()),
             dma((E,)), dma((E + 1, CB)),
         ],
         compiler_params=pltpu.CompilerParams(
             collective_id=0, has_side_effects=True, vmem_limit_bytes=min(room, 67043328 - (1 << 20))),
     )(*(pltpu.with_memory_space_constraint(a, pltpu.HBM) for a in (
         tokens, grad_hidden, routes.T, gates.T, weight, error, q_seed[0].T)))
+    return pl.pallas_call(
+        functools.partial(finish, chunk),
+        out_shape=(
+            jax.ShapeDtypeStruct((rows, width), BF16),
+            jax.ShapeDtypeStruct((1, 1, width, hidden), BF16),
+            jax.ShapeDtypeStruct((1, shard, hidden), F32),
+        ),
+        in_specs=[vmem] * 4,
+        out_specs=(hbm, hbm, hbm),
+        scratch_shapes=[
+            pltpu.VMEM((width, hidden), BF16),
+            pltpu.VMEM((shard, hidden), F32),
+            dma((2 + width // chunk,)),
+        ],
+        compiler_params=pltpu.CompilerParams(vmem_limit_bytes=16 << 20),
+    )(*parts)
 
 
 def solution(mesh):

time: 66.9 us -> 64 us (0.957)
  local copies, waits for them, and re-layouts: 2.76 us -> 0 us
    unnamed x3 -> x0, local copies, waits for them, and re-layouts: 2.76 us -> none
    pallas_call x1, Pallas kernels: 63.3 us -> 61.5 us  [body(): pl.pallas_call(functools.partial(kernel, (E, N, rp, chunk, gather_w, C, C...]
    pallas_call x0 -> x1, Pallas kernels: none -> 1.64 us  [body(): pl.pallas_call(functools.partial(finish, chunk), out_shape=(jax.ShapeDtyp...]
where the time goes in v4:
time: 64 us; the launch traced here: 63.8 us
  Pallas kernels  63.2 us (99%)
  between operations  0.64 us (1%)
    pallas_call x1, Pallas kernels, body(): pl.pallas_call(functools.partial(kernel, (E, N, rp, chunk, gather_w, C, C...  61.5 us
    pallas_call x1, Pallas kernels, body(): pl.pallas_call(functools.partial(finish, chunk), out_shape=(jax.ShapeDtyp...  1.64 us

profile of v4, /device:TPU:0, one launch (start us, length us, event | category | flops | bytes accessed | tf_op | source)
XLA Modules:
  0.0 63.8 jit_solution(10559770540224531061)
XLA Ops:
  0.6 61.5 %shard_map.94 = (bf16[128,1792]{1,0:T(8,128)(2,1)S(1)}, f32[1792,512]{1,0:T(8,128)S(1)}, bf16[1792,32]{1,0:T(8,128)(2,1)S(1)}, bf16[32,512]{1,0:T(8,128)(2,1)S(1)}) custom-call(bf16[128,1792]{1,0:T(8,128)(2,1)} %tok_hbm.1, bf16[128,2,512]{2,1,0:T(2,128)(2,1)} %gh_hbm.1, s32[2,128]{1,0:T(2,128)} %bitcast.8, f32[2,128]{1,0:T(2,128)} %bitcast.9, ...), custom_call_target="tpu_custom_call" | custom-call | tf_op jit(solution)/shard_map/pallas_call | solution.py:580
  62.2 1.6 %shard_map.95 = (bf16[128,1792]{1,0:T(8,128)(2,1)}, bf16[1,1,1792,512]{3,2,1,0:T(8,128)(2,1)}, f32[1,224,512]{2,1,0:T(8,128)}) custom-call(bf16[128,1792]{1,0:T(8,128)(2,1)S(1)} %get-tuple-element.7.gt_v, f32[1792,512]{1,0:T(8,128)S(1)} %get-tuple-element.8.merged, bf16[1792,32]{1,0:T(8,128)(2,1)S(1)} %get-tuple-element.9.bt_v, ...), custom_call_target="tpu_custom_call" | custom-call | tf_op jit(solution)/shard_map/pallas_call | solution.py:621

commit v5 on v4

--- a/solution.py
+++ b/solution.py
@@ -44,7 +44,7 @@
     (0, 0), (3, 4), (0, 1), (3, 5), (0, 2), (3, 6), (0, 3), (3, 7),
     (0, 4), (2, 4), (0, 5), (2, 5), (0, 6), (2, 6), (0, 7), (2, 7),
 )
-STOPS = (4, 7, 9, 11, 13, 15)
+STOPS = (4, 7, 8, 10, 12, 14)
 
 
 def slopes(pre_act):
@@ -87,8 +87,8 @@
            gt_out, merged, bt_v, q_out,
            tok_all, gh_raw, gh_sel, gh_all, rt_v, gt_v, gate_sel, gate_all, w_all, x_all, gp_all,
            err_v, merged_b, back, ret, q_v, q2, facc, fbuf, rsbuf, agbuf, tbuf,
-           in_s, tok_s, tok_r, gh_s, gh_r, gate_s, gate_r, w_s, w_r,
-           f_s, f_r, a_s, a_r, t_s, t_r, b_s, b_r):
+           hop_s, in_s, tok_s, tok_r, gh_s, gh_r, gate_s, gate_r, w_s, w_r,
+           f_s, f_r, a_s, a_r, t_s, t_r, t_x, b_s, b_r):
     E, N, rp, chunk, gather_w, C, CB = dims
     z = lax.axis_index("expert")
     me = lax.axis_index("dp")
@@ -109,10 +109,26 @@
         lax.fori_loop(start, size, step, 0)
 
     barrier = pltpu.get_barrier_semaphore()
-    for axis, size in (("expert", E), ("dp", N)):
-        for k in range(1, size):
-            pl.semaphore_signal(barrier, inc=1, device_id={axis: other(axis, size, k)},
+    stepped = E == len(PLAN) * 2 and N & (N - 1) == 0 and N.bit_length() <= E
+    bits = [1 << b for b in range(N.bit_length() - 1)]
+
+    def greet(sem):
+        for dirn in (1, -1):
+            @pl.when((z + dirn >= 0) & (z + dirn < E))
+            def _():
+                pl.semaphore_signal(sem, inc=1, device_id={"expert": z + dirn}, device_id_type=MESH)
+        for bit in bits:
+            pl.semaphore_signal(sem, inc=1, device_id={"dp": me + bit - 2 * bit * lax.rem(me // bit, 2)},
                                 device_id_type=MESH)
+
+    greeted = jnp.where((z == 0) | (z == E - 1), 1, 2) + len(bits)
+    if stepped:
+        greet(barrier)
+    else:
+        for axis, size in (("expert", E), ("dp", N)):
+            for k in range(1, size):
+                pl.semaphore_signal(barrier, inc=1, device_id={axis: other(axis, size, k)},
+                                    device_id_type=MESH)
 
     def w_rows(slot):
         return w_all.at[pl.ds(pl.multiple_of(slot * shard, 16), shard)] if gather_w else w_all
@@ -165,13 +181,13 @@
 
     partner = me + 1 - 2 * lax.rem(me, 2)
     half = N // 2
+    paired = N & (N - 1) == 0
 
     def cross(k):
         return me + 2 * (lax.bitwise_xor(me // 2, k) - me // 2)
 
-    for i in range(4):
-        loads[i].wait()
-    pl.semaphore_wait(barrier, E - 1 + N - 1)
+    loads[0].wait()
+    pl.semaphore_wait(barrier, greeted if stepped else E - 1 + N - 1)
 
     for d, dirn in enumerate((1, -1)):
         nb = z + dirn
@@ -179,9 +195,15 @@
         @pl.when((nb >= 0) & (nb < E))
         def _():
             loop(C, lambda c: tok_copy(z, c, nb, d).start(), 0)
+    for i in range(1, 4):
+        loads[i].wait()
     if gather_w:
-        loop(half, lambda k: w_copy(cross(k), me, k).start())
+        for k in range(1, half):
+            if not stepped or k in bits:
+                w_copy(cross(k), me, k).start()
         w_copy(partner, me, 0).start()
+    if stepped:
+        greet(hop_s.at[0])
 
     routes = rt_v[...]
     gates = gt_v[...]
@@ -190,7 +212,6 @@
         row = jnp.where(routes[0:1] == e, gates[0:1], jnp.where(routes[1:2] == e, gates[1:2], 0.0))
         gate_sel[e] = jnp.broadcast_to(row, (8, tokens))
     loop(E, pick_gate, 0)
-    each("expert", E, gate_copy, "start")
     gate_all[z] = gate_sel[z]
 
     loads[4].wait()
@@ -240,10 +261,10 @@
             code = jnp.where(k == n, table[n], code)
         return code
 
-    if E == len(PLAN) * 2:
-        acts(lambda low: [act(op) for op in PLAN[low][0]])
-    else:
-        loop(E, lambda k: gh_send(other("expert", E, k)))
+    if stepped:
+        pl.semaphore_wait(hop_s.at[0], greeted)
+        for n in range(1, max(E - 2, len(bits) - 1)):
+            greet(hop_s.at[n])
 
     loads[5].wait()
     loads[6].wait()
@@ -254,6 +275,19 @@
         facc[:, cols] = fold(lax.dot_general(
             q2[...], err_v[cols, :], NT, preferred_element_type=F32))
     loop(width // chunk, err_factor, 0)
+    if stepped:
+        for n in range(1, max(E - 2, len(bits) - 1)):
+            pl.semaphore_wait(hop_s.at[n], greeted)
+        if gather_w:
+            for k in range(1, half):
+                if k not in bits:
+                    w_copy(cross(k), me, k).start()
+    each("expert", E, gate_copy, "start")
+    if E == len(PLAN) * 2:
+        acts(lambda low: [act(op) for op in PLAN[low][0]])
+    else:
+        loop(E, lambda k: gh_send(other("expert", E, k)))
+
 
     def back_rows(c):
         return pl.ds(pl.multiple_of(c * back_part, 16), back_part)
@@ -395,8 +429,8 @@
         piece = agbuf.at[pl.ds(pl.multiple_of(slot * rp, 16), rp)]
         return rdma(piece, piece, a_s, a_r, "dp", p)
 
-    def t_copy(p, slot, k):
-        return rdma(tbuf.at[slot], tbuf.at[slot], t_s, t_r, "dp", p)
+    def t_copy(p, slot, sem):
+        return rdma(tbuf.at[slot], tbuf.at[slot], t_s, sem, "dp", p)
 
     def all_f():
         return rdma(rsbuf.at[pl.ds(0, N - 1)], rsbuf.at[pl.ds(0, N - 1)], f_s, f_r, "dp", partner)
@@ -405,8 +439,9 @@
         rest = agbuf.at[pl.ds(0, rp * (N - 1))]
         return rdma(rest, rest, a_s, a_r, "dp", partner)
 
-    def all_t():
-        return rdma(tbuf.at[pl.ds(0, N - 1)], tbuf.at[pl.ds(0, N - 1)], t_s, t_r, "dp", partner)
+    def all_t(count, sem):
+        slots = tbuf.at[pl.ds(0, count)]
+        return rdma(slots, slots, t_s, sem, "dp", partner)
 
     own = pl.ds(pl.multiple_of(me * rp, 16), rp)
     each("dp", N, f_copy, "start")
@@ -473,7 +508,11 @@
     all_a().wait_recv()
     factor = jnp.concatenate([agbuf[c * rank : (c + 1) * rank, :] for c in range(groups)], axis=1)
     tbuf[me] = jnp.dot(factor, merged_b[...], preferred_element_type=F32).astype(BF16)
-    each("dp", N, t_copy, "start")
+    if paired:
+        loop(half, lambda k: t_copy(cross(k), me, t_x).start())
+        t_copy(partner, me, t_r).start()
+    else:
+        loop(N, lambda k: t_copy(other("dp", N, k), me, t_r).start())
 
     if E == len(PLAN) * 2:
         planned(STOPS[1], STOPS[2])
@@ -484,6 +523,9 @@
     inverse = inverse_factor(gram, between)
     basis = fold(jnp.dot(halves(inverse), factor, preferred_element_type=F32))
     bt_v[...] = jnp.transpose(basis).astype(BF16)
+    if paired:
+        all_t(half - 1, t_x).wait_recv()
+        loop(half, lambda k: t_copy(partner, cross(k), t_r).start())
 
     if E == len(PLAN) * 2:
         planned(STOPS[-1], len(RELAYS))
@@ -511,7 +553,7 @@
         rdma(rest, rest, w_s, w_r.at[0], "dp", partner).wait_send()
     all_f().wait_send()
     all_a().wait_send()
-    all_t().wait_recv()
+    all_t(half if paired else N - 1, t_r).wait_recv()
     mean = jnp.sum(tbuf[...].astype(F32), axis=0) * (1.0 / N)
     q_out[...] = jnp.dot(inverse, mean, precision=HI, preferred_element_type=F32).astype(BF16)
 
@@ -535,7 +577,7 @@
         rdma(back.at[dest], ret.at[dest], b_s.at[dest], b_r.at[dest, 0], "expert",
              other("expert", E, 1)).wait_send()
     loop(E, sent)
-    all_t().wait_send()
+    all_t(N - 1, t_s).wait_send()
 
 
 def finish(chunk, gt_v, merged, bt_v, q_v, gt_hbm, err_hbm, wg_hbm, err_v, wg_v, sem):
@@ -610,9 +652,9 @@
             pltpu.VMEM((N, rp, 128), BF16),
             pltpu.VMEM((rp * N, 128), BF16),
             pltpu.VMEM((N, rank, hidden), BF16),
-            dma((7,)), dma((2, E)), dma((E, C)), dma(()), dma((E,)), dma(()), dma((E,)),
+            pltpu.SemaphoreType.REGULAR((2,)), dma((7,)), dma((2, E)), dma((E, C)), dma(()), dma((E,)), dma(()), dma((E,)),
             dma(()), dma((N,)), dma(()), dma(()), dma(()), dma(()), dma(()), dma(()),
-            dma((E,)), dma((E + 1, CB)),
+            dma(()), dma((E,)), dma((E + 1, CB)),
         ],
         compiler_params=pltpu.CompilerParams(
             collective_id=0, has_side_effects=True, vmem_limit_bytes=min(room, 67043328 - (1 << 20))),

time: 64 us -> 63 us (0.984)
  Pallas kernels: 63.2 us -> 62.2 us
    pallas_call x1, Pallas kernels: 61.5 us -> 60.6 us  [body(): pl.pallas_call(functools.partial(kernel, (E, N, rp, chunk, gather_w, C, C...]
where the time goes in v5:
time: 63 us; the launch traced here: 62.8 us
  Pallas kernels  62.2 us (99%)
  between operations  0.64 us (1%)
    pallas_call x1, Pallas kernels, body(): pl.pallas_call(functools.partial(kernel, (E, N, rp, chunk, gather_w, C, C...  60.6 us
    pallas_call x1, Pallas kernels, body(): pl.pallas_call(functools.partial(finish, chunk), out_shape=(jax.ShapeDtyp...  1.64 us

profile of v5, /device:TPU:0, one launch (start us, length us, event | category | flops | bytes accessed | tf_op | source)
XLA Modules:
  0.0 62.8 jit_solution(16583741870675635478)
XLA Ops:
  0.6 60.6 %shard_map.94 = (bf16[128,1792]{1,0:T(8,128)(2,1)S(1)}, f32[1792,512]{1,0:T(8,128)S(1)}, bf16[1792,32]{1,0:T(8,128)(2,1)S(1)}, bf16[32,512]{1,0:T(8,128)(2,1)S(1)}) custom-call(bf16[128,1792]{1,0:T(8,128)(2,1)} %tok_hbm.1, bf16[128,2,512]{2,1,0:T(2,128)(2,1)} %gh_hbm.1, s32[2,128]{1,0:T(2,128)} %bitcast.8, f32[2,128]{1,0:T(2,128)} %bitcast.9, ...), custom_call_target="tpu_custom_call" | custom-call | tf_op jit(solution)/shard_map/pallas_call | solution.py:622
  61.2 1.6 %shard_map.95 = (bf16[128,1792]{1,0:T(8,128)(2,1)}, bf16[1,1,1792,512]{3,2,1,0:T(8,128)(2,1)}, f32[1,224,512]{2,1,0:T(8,128)}) custom-call(bf16[128,1792]{1,0:T(8,128)(2,1)S(1)} %get-tuple-element.7.gt_v, f32[1792,512]{1,0:T(8,128)S(1)} %get-tuple-element.8.merged, bf16[1792,32]{1,0:T(8,128)(2,1)S(1)} %get-tuple-element.9.bt_v, ...), custom_call_target="tpu_custom_call" | custom-call | tf_op jit(solution)/shard_map/pallas_call | solution.py:663

commit v6 on v5

--- a/solution.py
+++ b/solution.py
@@ -97,6 +97,7 @@
     rank = q_hbm.shape[0]
     groups = width // 128
     part = tokens // C
+    paired = N & (N - 1) == 0
     back_part = tokens // CB
 
     def other(axis, size, k):
@@ -111,6 +112,13 @@
     barrier = pltpu.get_barrier_semaphore()
     stepped = E == len(PLAN) * 2 and N & (N - 1) == 0 and N.bit_length() <= E
     bits = [1 << b for b in range(N.bit_length() - 1)]
+
+    def spread(copy):
+        if paired:
+            for k in sorted(range(1, N), key=lambda k: (-(k // 2).bit_count(), -k)):
+                copy(lax.bitwise_xor(me, k), me, k).start()
+        else:
+            each("dp", N, copy, "start")
 
     def greet(sem):
         for dirn in (1, -1):
@@ -181,7 +189,6 @@
 
     partner = me + 1 - 2 * lax.rem(me, 2)
     half = N // 2
-    paired = N & (N - 1) == 0
 
     def cross(k):
         return me + 2 * (lax.bitwise_xor(me // 2, k) - me // 2)
@@ -444,7 +451,7 @@
         return rdma(slots, slots, t_s, sem, "dp", partner)
 
     own = pl.ds(pl.multiple_of(me * rp, 16), rp)
-    each("dp", N, f_copy, "start")
+    spread(f_copy)
     rsbuf[me] = fbuf[own, :]
 
     if E == len(PLAN) * 2:
@@ -498,11 +505,18 @@
         relays(1, E - 1, 0, CB // 2)
     all_f().wait_recv()
     agbuf[own, :] = (jnp.sum(rsbuf[...].astype(F32), axis=0) * (1.0 / N)).astype(BF16)
-    each("dp", N, a_copy, "start")
-    loop(width // chunk, merge, 0)
-
+    spread(a_copy)
     if E == len(PLAN) * 2:
-        planned(STOPS[0], STOPS[1])
+        cut = width // chunk // 2 + 1
+        planned(STOPS[0], STOPS[0] + 1)
+        loop(cut, merge, 0)
+        planned(STOPS[0] + 1, STOPS[0] + 2)
+        loop(width // chunk, merge, cut)
+    else:
+        loop(width // chunk, merge, 0)
+
+    if E == len(PLAN) * 2:
+        planned(STOPS[0] + 2, STOPS[1])
     else:
         relays(1, E - 1, CB // 2, CB + lag)
     all_a().wait_recv()

time: 63 us -> 62 us (0.984)
  Pallas kernels: 62.2 us -> 61.2 us
    pallas_call x1, Pallas kernels: 60.6 us -> 59.5 us  [body(): pl.pallas_call(functools.partial(kernel, (E, N, rp, chunk, gather_w, C, C...]
where the time goes in v6:
time: 62 us; the launch traced here: 61.8 us
  Pallas kernels  61.2 us (99%)
  between operations  0.64 us (1%)
    pallas_call x1, Pallas kernels, body(): pl.pallas_call(functools.partial(kernel, (E, N, rp, chunk, gather_w, C, C...  59.5 us
    pallas_call x1, Pallas kernels, body(): pl.pallas_call(functools.partial(finish, chunk), out_shape=(jax.ShapeDtyp...  1.64 us

profile of v6, /device:TPU:0, one launch (start us, length us, event | category | flops | bytes accessed | tf_op | source)
XLA Modules:
  0.0 61.8 jit_solution(4929503273478395220)
XLA Ops:
  0.6 59.5 %shard_map.94 = (bf16[128,1792]{1,0:T(8,128)(2,1)S(1)}, f32[1792,512]{1,0:T(8,128)S(1)}, bf16[1792,32]{1,0:T(8,128)(2,1)S(1)}, bf16[32,512]{1,0:T(8,128)(2,1)S(1)}) custom-call(bf16[128,1792]{1,0:T(8,128)(2,1)} %tok_hbm.1, bf16[128,2,512]{2,1,0:T(2,128)(2,1)} %gh_hbm.1, s32[2,128]{1,0:T(2,128)} %bitcast.8, f32[2,128]{1,0:T(2,128)} %bitcast.9, ...), custom_call_target="tpu_custom_call" | custom-call | tf_op jit(solution)/shard_map/pallas_call | solution.py:636
  60.2 1.6 %shard_map.95 = (bf16[128,1792]{1,0:T(8,128)(2,1)}, bf16[1,1,1792,512]{3,2,1,0:T(8,128)(2,1)}, f32[1,224,512]{2,1,0:T(8,128)}) custom-call(bf16[128,1792]{1,0:T(8,128)(2,1)S(1)} %get-tuple-element.7.gt_v, f32[1792,512]{1,0:T(8,128)S(1)} %get-tuple-element.8.merged, bf16[1792,32]{1,0:T(8,128)(2,1)S(1)} %get-tuple-element.9.bt_v, ...), custom_call_target="tpu_custom_call" | custom-call | tf_op jit(solution)/shard_map/pallas_call | solution.py:677
